TPU v7x, 8 devices: a whole 2x2x1 slice. The times are simulated.
8 devices in a mesh: data: 8 (over z, y, x, core).
Axes of the slice: x: 2, y: 2, z: 1, core: 2. Of those that a mesh axis runs over, the one named last changes fastest.
Arguments:
- tokens: bfloat16 [8192, 768], P('data')
- w_in: bfloat16 [768, 3072], replicated
- w_out: bfloat16 [3072, 768], replicated
- task_heads: bfloat16 [4, 768, 3], replicated
- labels: int32 [4, 8192], P(None, 'data')
- label_mask: int32 [4, 8192], P(None, 'data')
Outputs:
- output 1: float32 [4], replicated
- output 2: float32 [2359296], P('data')
- output 3: float32 [2359296], P('data')
All inputs are finite; a program needn't handle non-finite values.
Results may differ from a plain program's by a relative error of at most 0.00839703.
Values are sent between devices in bfloat16 or wider.
A program may use at most 1 GiB of HBM per device.

v0:
```python
import jax
import jax.numpy as jnp
from jax import lax
from jax.sharding import PartitionSpec as P

SOLVER_STEPS = 20


def device_grads(x_loc, w_in, w_out, task_heads, lab_loc, mask_loc):
    pre_act = jnp.dot(x_loc, w_in, preferred_element_type=jnp.float32)
    act_out, gelu_slope = jax.jvp(jax.nn.gelu, (pre_act,), (jnp.ones_like(pre_act),))
    act_bf = act_out.astype(jnp.bfloat16)
    residual = x_loc.astype(jnp.float32) + jnp.dot(act_bf, w_out, preferred_element_type=jnp.float32)
    z_bf = residual.astype(jnp.bfloat16)
    logits = jnp.einsum("bd,tdc->tbc", z_bf, task_heads, preferred_element_type=jnp.float32)
    soft_prob = jax.nn.softmax(logits, axis=-1)
    class_ids = jnp.arange(logits.shape[-1])
    onehot = (lab_loc[:, :, None] == class_ids).astype(jnp.float32)
    d_logit = (mask_loc[:, :, None].astype(jnp.float32) * (soft_prob - onehot)).astype(jnp.bfloat16)
    d_resid = jnp.einsum("tbc,tdc->tbd", d_logit, task_heads, preferred_element_type=jnp.float32).astype(jnp.bfloat16)
    grad_w_out = jnp.einsum("bf,tbd->tfd", act_bf, d_resid, preferred_element_type=jnp.float32)
    d_act = jnp.einsum("tbd,fd->tbf", d_resid, w_out, preferred_element_type=jnp.float32)
    d_pre = (d_act * gelu_slope[None]).astype(jnp.bfloat16)
    grad_w_in = jnp.einsum("bd,tbf->tdf", x_loc, d_pre, preferred_element_type=jnp.float32)
    return grad_w_in, grad_w_out


def gram_of(grad_rows):
    return jnp.einsum("tk,sk->ts", grad_rows, grad_rows, precision=lax.Precision.HIGHEST, preferred_element_type=jnp.float32)


def solve_weights(gram_mat):
    num_tasks = gram_mat.shape[0]
    step_scale = jnp.trace(gram_mat) / num_tasks

    def solver_step(step_idx, weights):
        pull_vec = (gram_mat * weights[None, :]).sum(axis=1)
        raised = weights * jnp.exp(-pull_vec / step_scale)
        return raised / raised.sum()

    init_weights = jnp.full((num_tasks,), 1.0 / num_tasks, jnp.float32)
    return lax.fori_loop(0, SOLVER_STEPS, solver_step, init_weights)


def solution(mesh):
    group_size = mesh.shape["data"]

    def local_step(x_loc, w_in, w_out, task_heads, lab_loc, mask_loc):
        num_tasks = task_heads.shape[0]
        label_count = lax.psum(mask_loc.sum(axis=1), "data")
        inv_count = 1.0 / jnp.maximum(label_count, 1).astype(jnp.float32)
        grad_w_in, grad_w_out = device_grads(x_loc, w_in, w_out, task_heads, lab_loc, mask_loc)
        shards = []
        for grad_full in (grad_w_in, grad_w_out):
            scaled = (grad_full.reshape(num_tasks, group_size, -1) * inv_count[:, None, None]).astype(jnp.bfloat16)
            arrived = lax.all_to_all(scaled, "data", 1, 1, tiled=True)
            shards.append(arrived.sum(axis=1, dtype=jnp.float32))
        gram_mat = lax.psum(gram_of(shards[0]) + gram_of(shards[1]), "data")
        weights = solve_weights(gram_mat)
        grad_in = (weights[:, None] * shards[0]).sum(axis=0)
        grad_out = (weights[:, None] * shards[1]).sum(axis=0)
        return weights, grad_in, grad_out

    return jax.shard_map(local_step, mesh=mesh, in_specs=(P("data", None), P(), P(), P(), P(None, "data"), P(None, "data")), out_specs=(P(), P("data"), P("data")), check_vma=False)
```

profile of v0, /device:TPU:0, one launch (start us, length us, event | category | flops | bytes accessed | tf_op | source)
XLA Modules:
  0.0 892.7 jit_solution(18173054244948896951)
XLA Ops:
  0.6 1.4 fusion.24
  2.1 17.4 %fusion.9 = (f32[1024,3072]{1,0:T(8,128)}, f32[1024,3072]{1,0:T(8,128)}) fusion(bf16[1024,768]{1,0:T(8,128)(2,1)} %param.8, bf16[768,3072]{1,0:T(8,128)(2,1)} %param.9), kind=kOutput, calls=%fused_computation.22 | convolution fusion | flops 4882169856 | bytes 31457280 | tf_op jit(solution)/shard_map/dot_general | solution.py:10
  19.6 13.8 %fusion.25 = (f32[4,1024]{1,0:T(4,128)S(1)}, f32[4,1024,3]{1,0,2:T(4,128)S(1)}) fusion(bf16[4,768,3]{1,0,2:T(4,128)(2,1)S(1)} %copy-done, bf16[3072,768]{1,0:T(8,128)(2,1)} %param.10, bf16[1024,768]{1,0:T(8,128)(2,1)S(1)} %copy-done.6, f32[1024,3072]{1,0:T(8,128)} %get-tuple-element.60), kind=kOutput, calls=%fused_computation.47 | convolution fusion | flops 4881391616 | bytes 18958336 | tf_op jit(solution)/shard_map/bd,tdc->tbc/dot_general | solution.py:15
  33.4 1.8 convolution_convert_fusion
  35.3 2.6 copy-done.2
  37.9 28.0 %convolution_bitcast_fusion = f32[4,3072,768]{1,2,0:T(8,128)} fusion(bf16[4,1024,768]{2,1,0:T(8,128)(2,1)S(1)} %convolution_convert_fusion, f32[1024,3072]{1,0:T(8,128)} %get-tuple-element.60), kind=kOutput, calls=%fused_computation.11 | convolution fusion | flops 19355664384 | bytes 56623104 | tf_op jit(solution)/shard_map/bf,tbd->tfd/dot_general | solution.py:21
  65.9 36.7 %copy.33 = f32[4,3072,768]{2,1,0:T(8,128)} copy(f32[4,3072,768]{1,2,0:T(8,128)} %convolution_bitcast_fusion) | data formatting | bytes 75497472 | tf_op jit(solution)/shard_map/bf,tbd->tfd/transpose | solution.py:21
  102.6 36.0 %reshape.22 = f32[4,8,294912]{2,1,0:T(8,128)} reshape(f32[4,3072,768]{2,1,0:T(8,128)} %copy.33) | data formatting | bytes 75497472 | tf_op jit(solution)/shard_map/reshape | solution.py:55
  138.7 28.7 %multiply_convert_fusion.clone.4 = bf16[4,1024,3072]{2,1,0:T(8,128)(2,1)} fusion(bf16[4,1024,768]{2,1,0:T(8,128)(2,1)} %copy-done.2, f32[1024,3072]{1,0:T(8,128)} %get-tuple-element.59, bf16[3072,768]{1,0:T(8,128)(2,1)} %param.10), kind=kOutput, calls=%fused_computation.4.clone.clone.clone.1 | convolution fusion | flops 19352518656 | bytes 48758784 | tf_op jit(solution)/shard_map/tbd,fd->tbf/dot_general | solution.py:22
  167.4 29.8 %convolution_bitcast_fusion.1 = f32[4,768,3072]{1,2,0:T(8,128)} fusion(bf16[1024,768]{1,0:T(8,128)(2,1)S(1)} %copy-done.6, bf16[4,1024,3072]{2,1,0:T(8,128)(2,1)} %multiply_convert_fusion.clone.4), kind=kOutput, calls=%fused_computation.12 | convolution fusion | flops 19327352832 | bytes 64487424 | tf_op jit(solution)/shard_map/bd,tbf->tdf/dot_general | solution.py:24
  197.2 36.8 %copy.30 = f32[4,768,3072]{2,1,0:T(8,128)} copy(f32[4,768,3072]{1,2,0:T(8,128)} %convolution_bitcast_fusion.1) | data formatting | bytes 75497472 | tf_op jit(solution)/shard_map/bd,tbf->tdf/transpose | solution.py:24
  233.9 35.7 %reshape.21 = f32[4,8,294912]{2,1,0:T(8,128)} reshape(f32[4,768,3072]{2,1,0:T(8,128)} %copy.30) | data formatting | bytes 75497472 | tf_op jit(solution)/shard_map/reshape | solution.py:55
  269.6 25.2 %psum.14 = s32[4]{0:T(128)S(1)} all-reduce(s32[4]{0:T(128)S(1)} %copy-done.5), channel_id=1, replica_groups=mesh['data'=8] {'data'}, use_global_device_ids=true, to_apply=%region_3.0 | all-reduce | flops 4 | bytes 32 | tf_op jit(solution)/shard_map/psum | solution.py:50
  294.8 30.6 %multiply_convert_fusion.1 = (bf16[4,8,294912]{2,1,0:T(8,128)(2,1)}, bf16[4,8,294912]{2,1,0:T(8,128)(2,1)S(1)}) fusion(f32[4,8,294912]{2,1,0:T(8,128)} %reshape.22, f32[4]{0:T(128)S(1)} %convert_divide_fusion, f32[4,8,294912]{2,1,0:T(8,128)} %reshape.21), kind=kLoop, calls=%fused_computation.6 | loop fusion | flops 37748736 | bytes 113246224 | tf_op jit(solution)/shard_map/convert_element_type | solution.py:55
  325.5 35.7 %copy.31 = bf16[4,8,294912]{2,0,1:T(4,128)(2,1)} copy(bf16[4,8,294912]{2,1,0:T(8,128)(2,1)S(1)} %get-tuple-element.56) | data formatting | bytes 37748736 | tf_op jit(solution)/shard_map/convert_element_type | solution.py:55
  361.2 4.6 all-to-all-start
  365.8 24.5 %copy.34 = bf16[4,8,294912]{2,0,1:T(4,128)(2,1)} copy(bf16[4,8,294912]{2,1,0:T(8,128)(2,1)} %get-tuple-element.55) | data formatting | bytes 37748736 | tf_op jit(solution)/shard_map/convert_element_type | solution.py:55
  390.3 181.9 %all-to-all-done = bf16[4,8,294912]{2,0,1:T(4,128)(2,1)} async-done(((bf16[4,8,294912]{2,0,1:T(4,128)(2,1)}), bf16[4,8,294912]{2,0,1:T(4,128)(2,1)}, u32[]{:S(2)}, u32[]{:S(2)}) %all-to-all-start) | async-done | bytes 18874400 | tf_op jit(solution)/shard_map/all_to_all | solution.py:56
  572.3 4.6 all-to-all-start.1
  576.9 12.9 %convert_reduce_fusion.1 = f32[4,294912]{1,0:T(4,128)} fusion(bf16[4,8,294912]{2,0,1:T(4,128)(2,1)} %all-to-all-done), kind=kLoop, calls=%fused_computation.7 | loop fusion | flops 17694720 | bytes 23592960 | tf_op jit(solution)/shard_map/reduce_sum | solution.py:57
  589.8 24.4 %fusion.26 = f32[4,4]{1,0:T(4,128)S(1)} fusion(f32[4,294912]{1,0:T(4,128)} %convert_reduce_fusion.1), kind=kOutput, calls=%fused_computation.48 | convolution fusion | flops 56623104 | bytes 4718656 | tf_op jit(solution)/shard_map/tk,sk->ts/dot_general | solution.py:29
  614.2 169.1 %all-to-all-done.1 = bf16[4,8,294912]{2,0,1:T(4,128)(2,1)} async-done(((bf16[4,8,294912]{2,0,1:T(4,128)(2,1)}), bf16[4,8,294912]{2,0,1:T(4,128)(2,1)}, u32[]{:S(2)}, u32[]{:S(2)}) %all-to-all-start.1) | async-done | bytes 18874400 | tf_op jit(solution)/shard_map/all_to_all | solution.py:56
  783.3 12.9 %convert_reduce_fusion = f32[4,294912]{1,0:T(4,128)} fusion(bf16[4,8,294912]{2,0,1:T(4,128)(2,1)} %all-to-all-done.1), kind=kLoop, calls=%fused_computation.5 | loop fusion | flops 17694720 | bytes 23592960 | tf_op jit(solution)/shard_map/reduce_sum | solution.py:57
  796.2 25.0 %convolution_add_fusion = f32[4,4]{1,0:T(4,128)S(1)} fusion(f32[4,4]{1,0:T(4,128)S(1)} %fusion.26, f32[4,294912]{1,0:T(4,128)} %convert_reduce_fusion), kind=kOutput, calls=%fused_computation.34 | convolution fusion | flops 56623120 | bytes 4718720 | tf_op jit(solution)/shard_map/tk,sk->ts/dot_general | solution.py:29
  821.2 22.4 %psum.15 = f32[4,4]{1,0:T(4,128)S(1)} all-reduce(f32[4,4]{1,0:T(4,128)S(1)} %convolution_add_fusion), channel_id=1, replica_groups=mesh['data'=8] {'data'}, use_global_device_ids=true, to_apply=%region_6.0 | all-reduce | flops 16 | bytes 128 | tf_op jit(solution)/shard_map/psum | solution.py:58
  844.9 28.4 %while.11 = (s32[]{:T(128)}, f32[4]{0:T(128)S(1)}, f32[4,4]{1,0:T(4,128)S(1)}, f32[]{:T(128)}, s32[]{:T(128)}, /*index=5*/s32[]{:T(128)}) while((s32[]{:T(128)}, f32[4]{0:T(128)S(1)}, f32[4,4]{1,0:T(4,128)S(1)}, f32[]{:T(128)}, s32[]{:T(128)}, /*index=5*/s32[]{:T(128)}) %tuple.34), condition=%wide.region_11.12_spmd.clone, body=%wide.region_8.11_spmd.clone.sunk | while | flops 58 | bytes 300 | solution.py:42
  845.6 0.6 broadcast_divide_fusion.2
  846.4 0.6 fusion.46
  847.0 0.6 broadcast_divide_fusion.2
  848.5 0.6 broadcast_divide_fusion.2
  849.9 0.6 broadcast_divide_fusion.2
  851.3 0.6 broadcast_divide_fusion.2
  852.7 0.6 broadcast_divide_fusion.2
  854.1 0.6 broadcast_divide_fusion.2
  855.6 0.6 broadcast_divide_fusion.2
  857.0 0.6 broadcast_divide_fusion.2
  858.4 0.6 broadcast_divide_fusion.2
  859.8 0.6 broadcast_divide_fusion.2
  861.2 0.6 broadcast_divide_fusion.2
  862.7 0.6 broadcast_divide_fusion.2
  864.1 0.6 broadcast_divide_fusion.2
  865.5 0.6 broadcast_divide_fusion.2
  866.9 0.6 broadcast_divide_fusion.2
  868.3 0.6 broadcast_divide_fusion.2
  869.8 0.6 broadcast_divide_fusion.2
  871.2 0.6 broadcast_divide_fusion.2
  872.6 0.6 broadcast_divide_fusion.2
  873.3 19.2 %multiply_reduce_fusion.1 = (f32[294912]{0:T(1024)}, f32[294912]{0:T(1024)}) fusion(f32[4,294912]{1,0:T(4,128)} %convert_reduce_fusion, f32[4]{0:T(128)S(1)} %get-tuple-element.22, f32[4,294912]{1,0:T(4,128)} %convert_reduce_fusion.1), kind=kLoop, calls=%fused_computation.26 | loop fusion | flops 4128768 | bytes 11796496 | tf_op jit(solution)/shard_map/reduce_sum | solution.py:61
  (77 shorter events, 14.9 us)
Async XLA Ops:
  0.6 18.9 %copy-start = (bf16[4,768,3]{1,0,2:T(4,128)(2,1)S(1)}, bf16[4,768,3]{1,0,2:T(4,128)(2,1)}, u32[]{:S(2)}) copy-start(bf16[4,768,3]{1,0,2:T(4,128)(2,1)} %param.11) | copy-start | bytes 55300
  2.1 17.5 %copy-start.6 = (bf16[1024,768]{1,0:T(8,128)(2,1)S(1)}, bf16[1024,768]{1,0:T(8,128)(2,1)}, u32[]{:S(2)}) copy-start(bf16[1024,768]{1,0:T(8,128)(2,1)} %param.8) | copy-start | bytes 4718596
  19.5 13.8 %copy-start.4 = (s32[4,1024]{1,0:T(4,128)S(1)}, s32[4,1024]{1,0:T(4,128)}, u32[]{:S(2)}) copy-start(s32[4,1024]{1,0:T(4,128)} %param.12) | copy-start | bytes 49156
  35.3 2.6 copy-start.2
  233.9 35.7 %copy-start.5 = (s32[4]{0:T(128)S(1)}, s32[4]{0:T(128)}, u32[]{:S(2)}) copy-start(s32[4]{0:T(128)} %get-tuple-element.53) | copy-start | bytes 52
  361.2 211.1 %all-to-all-start = ((bf16[4,8,294912]{2,0,1:T(4,128)(2,1)}), bf16[4,8,294912]{2,0,1:T(4,128)(2,1)}, u32[]{:S(2)}, u32[]{:S(2)}) async-start(bf16[4,8,294912]{2,0,1:T(4,128)(2,1)} %copy.31), calls=%async_computation | async-start | bytes 37748736 | tf_op jit(solution)/shard_map/all_to_all | solution.py:56
  572.3 211.1 %all-to-all-start.1 = ((bf16[4,8,294912]{2,0,1:T(4,128)(2,1)}), bf16[4,8,294912]{2,0,1:T(4,128)(2,1)}, u32[]{:S(2)}, u32[]{:S(2)}) async-start(bf16[4,8,294912]{2,0,1:T(4,128)(2,1)} %copy.34), calls=%async_computation.1 | async-start | bytes 37748736 | tf_op jit(solution)/shard_map/all_to_all | solution.py:56
  783.3 109.2 %copy-start.1 = (bf16[4,768,3]{1,0,2:T(4,128)(2,1)S(1)}, bf16[4,768,3]{1,0,2:T(4,128)(2,1)}, u32[]{:S(2)}) copy-start(bf16[4,768,3]{1,0,2:T(4,128)(2,1)} %param.11) | copy-start | bytes 55300
  873.3 19.3 %copy-start.3 = (f32[4]{0:T(128)}, f32[4]{0:T(128)S(1)}, u32[]{:S(2)}) copy-start(f32[4]{0:T(128)S(1)} %get-tuple-element.22) | copy-start | bytes 52
where the time goes:
time: 898 us; the launch traced here: 893 us
  waiting for transfers between devices  351 us (39%)
  local copies, waits for them, and re-layouts  208 us (23%)
  matrix products  169 us (19%)
  other arithmetic  106 us (12%)
  blocking collectives  47.6 us (5%)
  starting transfers between devices  9.27 us (1%)
    all_to_all x2, waiting for transfers between devices, local_step(): arrived = lax.all_to_all(scaled, 'data', 1, 1, tiled=True)  351 us
    reshape x2, local copies, waits for them, and re-layouts, local_step(): grad_full.reshape(num_tasks, group_size, -1) * inv_count[:, None, None]  71.7 us
    convert_element_type x2, local copies, waits for them, and re-layouts, local_step(): (grad_full.reshape(num_tasks, group_size, -1) * inv_count[:, None, None])...  60.2 us
    dot_general x2, matrix products, gram_of(): jnp.einsum('tk,sk->ts', grad_rows, grad_rows, precision=lax.Precision.HIG...  49.4 us
    transpose x1, local copies, waits for them, and re-layouts, device_grads(): jnp.einsum('bd,tbf->tdf', x_loc, d_pre, preferred_element_type=jnp.float32)  36.8 us
    transpose x1, local copies, waits for them, and re-layouts, device_grads(): jnp.einsum('bf,tbd->tfd', act_bf, d_resid, preferred_element_type=jnp.flo...  36.7 us
    convert_element_type x1, other arithmetic, local_step(): (grad_full.reshape(num_tasks, group_size, -1) * inv_count[:, None, None])...  30.6 us
    dot_general x1, matrix products, device_grads(): jnp.einsum('bd,tbf->tdf', x_loc, d_pre, preferred_element_type=jnp.float32)  29.8 us
  transfers between devices with their start and end apart: 2, of which 2 were waited for; matrix products, arithmetic and copies ran while one was open for 7% of the time, Pallas kernels for 0%

commit v1 on v0

v1 whole, which is shorter than its diff:
```python
import jax
import jax.numpy as jnp
from jax import lax
from jax.experimental import pallas as pl
from jax.experimental.pallas import tpu as pltpu
from jax.sharding import PartitionSpec as P

SOLVER_STEPS = 20
MESH = pl.DeviceIdType.MESH
F32, BF16 = jnp.float32, jnp.bfloat16
NUM_DEV = 8
TASKS = 4
CLASSES = 3
TOK = 1024
DIM = 768
HIDDEN = 3072
HID = HIDDEN // NUM_DEV
FEAT = DIM // NUM_DEV
HEAD_ROWS = 32
CHUNK = 768
ROWS = 512
PAIRS = [(t, s) for t in range(TASKS) for s in range(t, TASKS)]
GELU_C = 0.7978845608028654
GELU_K = 0.044715


def dot_nn(a, b):
    return lax.dot_general(a, b, (((1,), (0,)), ((), ())), preferred_element_type=F32)


def dot_nt(a, b):
    return lax.dot_general(a, b, (((1,), (1,)), ((), ())), preferred_element_type=F32)


def lanes(row, width):
    return jnp.concatenate([row] * (width // row.shape[1]), axis=1)


def gelu_value(p):
    return p * (0.5 * (1.0 + jnp.tanh(GELU_C * (p + GELU_K * (p * p * p)))))


def gelu_both(p):
    sq = p * p
    th = jnp.tanh(GELU_C * (p + GELU_K * (sq * p)))
    cdf = 0.5 * (1.0 + th)
    slope = cdf + (0.5 * p) * ((1.0 - th * th) * (GELU_C * (1.0 + (3.0 * GELU_K) * sq)))
    return p * cdf, slope


def kernel(x_hbm, w_in_hbm, w_out_hbm, head_ref, lab_ref, mask_ref, alpha_ref, out1_hbm, out2_hbm,
           xs, w1, w2, w1j, w1t, w2j, abuf, zacc, ef, es, etok, hm, act_t, slope_t, dz, q_t, acc1, acc2,
           cnt, inv, gram, gsend, grecv, stage1, stage2,
           x_send, x_recv, e_send, e_recv, c_send, c_recv, g_send, g_recv, o_send, o_recv, l_sem):
    me = lax.axis_index("data")
    core = lax.rem(me, 2)
    cx = lax.rem(lax.div(me, 2), 2)
    cy = lax.div(me, 4)

    def flip(v, b):
        return v + b - 2 * v * b

    def peer(slot):
        hop = slot // 2
        first, second = (1 if hop in (1, 3) else 0), (1 if hop in (2, 3) else 0)
        bx = first * (1 - core) + second * core
        by = first * core + second * (1 - core)
        bc = slot % 2
        return flip(cx, bx) * 2 + flip(cy, by) * 4 + flip(core, jnp.int32(bc))

    def remote(src, dst, send, recv, dev):
        return pltpu.make_async_remote_copy(src_ref=src, dst_ref=dst, send_sem=send, recv_sem=recv, device_id=(dev,), device_id_type=MESH)

    def x_copy(src_slot, dst_slot):
        dev = {1: 1, 2: 2, 4: 4, 3: 1, 5: 1, 6: 4, 7: 1}[dst_slot]
        return remote(xs.at[src_slot], xs.at[dst_slot], x_send.at[dst_slot], x_recv.at[dst_slot], peer(dev))

    def e_copy(slot):
        return remote(es.at[0], es.at[slot], e_send.at[slot], e_recv.at[slot], peer(slot))

    def c_copy(slot):
        return remote(cnt.at[0], cnt.at[slot], c_send.at[slot], c_recv.at[slot], peer(slot))

    def local(src, dst, i):
        return pltpu.make_async_copy(src, dst, l_sem.at[i])

    nchunk = HIDDEN // CHUNK
    load_x = local(x_hbm, xs.at[0], 0)
    load_w1 = [local(w_in_hbm.at[:, pl.ds(CHUNK * i, CHUNK)], w1.at[i], 1 + i) for i in range(nchunk)]
    load_w2 = [local(w_out_hbm.at[pl.ds(CHUNK * i, CHUNK), :], w2.at[i], 1 + nchunk + i) for i in range(nchunk)]
    load_w1j = local(w_in_hbm.at[:, pl.ds(pl.multiple_of(me * HID, HID), HID)], w1j, 1 + 2 * nchunk)
    load_w2j = local(w_out_hbm.at[pl.ds(pl.multiple_of(me * HID, HID), HID), :], w2j, 2 + 2 * nchunk)
    load_x.start()
    for i in range(nchunk):
        load_w1[i].start()
        load_w2[i].start()
    load_w1j.start()
    load_w2j.start()

    counts = jnp.sum(mask_ref[...].astype(F32), axis=1, keepdims=True)
    cnt[0, 0:TASKS, :] = jnp.broadcast_to(counts, (TASKS, 128))
    cnt[0, TASKS:8, :] = jnp.zeros((8 - TASKS, 128), F32)
    head = head_ref[...].astype(F32)
    row_task = lax.rem(lax.broadcasted_iota(jnp.int32, (HEAD_ROWS, DIM), 0), 8)
    for t in range(TASKS):
        hm[t] = jnp.where(row_task == t, head, 0.0).astype(BF16)

    barrier = pltpu.get_barrier_semaphore()
    for s in range(1, NUM_DEV):
        pl.semaphore_signal(barrier, inc=1, device_id=(peer(s),), device_id_type=MESH)
    pl.semaphore_wait(barrier, NUM_DEV - 1)

    load_x.wait()
    x_copy(0, 1).start()
    x_copy(0, 2).start()
    for s in range(1, NUM_DEV):
        c_copy(s).start()

    zacc[...] = xs[0].astype(F32)
    for c in load_w1 + load_w2:
        c.wait()

    def forward(i, carry):
        h = lax.div(i, TOK // ROWS)
        r = pl.ds(pl.multiple_of(lax.rem(i, TOK // ROWS) * ROWS, ROWS), ROWS)
        abuf[...] = gelu_value(dot_nn(xs[0, r, :], w1[h])).astype(BF16)
        zacc[r, :] += dot_nn(abuf[...], w2[h])
        return carry

    lax.fori_loop(0, nchunk * (TOK // ROWS), forward, 0)

    ef[...] = jnp.zeros_like(ef)
    for r in range(TOK // ROWS):
        cols = slice(r * ROWS, (r + 1) * ROWS)
        logits = dot_nt(head_ref[...], zacc[cols, :].astype(BF16))
        l = [logits[8 * c:8 * c + TASKS] for c in range(CLASSES)]
        top = jnp.maximum(jnp.maximum(l[0], l[1]), l[2])
        ex = [jnp.exp(v - top) for v in l]
        total = ex[0] + ex[1] + ex[2]
        lab = lab_ref[:, cols]
        m = mask_ref[:, cols].astype(F32)
        for c in range(CLASSES):
            ef[8 * c:8 * c + TASKS, cols] = m * (ex[c] / total - (lab == c).astype(F32))
    es[0] = ef[...].astype(BF16)

    acc1[...] = jnp.zeros_like(acc1)
    acc2[...] = jnp.zeros_like(acc2)
    load_w1j.wait()
    load_w2j.wait()
    w1t[...] = w1j[...].astype(F32).T.astype(BF16)

    for s in range(1, NUM_DEV):
        e_copy(s).start()
    total_cnt = cnt[0]
    for s in range(1, NUM_DEV):
        c_copy(s).wait_recv()
        total_cnt = total_cnt + cnt[s]
    inv[...] = lanes(1.0 / jnp.maximum(total_cnt, 1.0), DIM)

    def shard(s, carry):
        for k in range(1, NUM_DEV):
            @pl.when(s == k)
            def _():
                x_copy(0, k).wait_recv()
                e_copy(k).wait_recv()
                if k == 1:
                    x_copy(0, 2).wait_send()
                    x_copy(0, 4).start()
                if k in (2, 4, 6):
                    x_copy(k, k + 1).start()
                if k == 2:
                    x_copy(2, 6).start()

        etok[...] = es[s].astype(F32).T.astype(BF16)

        def preact(i, c):
            r = pl.ds(pl.multiple_of(i * ROWS, ROWS), ROWS)
            a, sl = gelu_both(dot_nt(w1t[...], xs[s, r, :]))
            act_t[:, r] = a.astype(BF16)
            slope_t[:, r] = sl
            return c

        lax.fori_loop(0, TOK // ROWS, preact, 0)

        def task(t, c):
            scale = inv[pl.ds(t, 1), :]
            dz[...] = dot_nn(etok[...], hm[t]).astype(BF16)
            q_t[...] = (dot_nt(w2j[...], dz[...]) * slope_t[...]).astype(BF16)
            acc2[t] += (dot_nn(act_t[...], dz[...]) * scale).astype(BF16).astype(F32)
            acc1[t] += (dot_nn(q_t[...], xs[s]) * scale).astype(BF16).astype(F32)
            return c

        lax.fori_loop(0, TASKS, task, 0)
        return carry

    lax.fori_loop(0, NUM_DEV, shard, 0)

    def gram_rows(i, sums):
        r = pl.ds(pl.multiple_of(i * 8, 8), 8)
        out = list(sums)
        for acc in (acc1, acc2):
            for c in range(DIM // 128):
                g = [acc[t, r, 128 * c:128 * c + 128] for t in range(TASKS)]
                for k, (t, u) in enumerate(PAIRS):
                    out[k] = out[k] + g[t] * g[u]
        return tuple(out)

    sums = lax.fori_loop(0, HID // 8, gram_rows, tuple(jnp.zeros((8, 128), F32) for _ in PAIRS))
    for k in range(len(PAIRS)):
        gram[me, k:k + 1, :] = jnp.broadcast_to(jnp.sum(sums[k]), (1, 128))
    gram[me, len(PAIRS):16, :] = jnp.zeros((16 - len(PAIRS), 128), F32)

    def gram_copy(s, block):
        return remote(gram.at[block], gram.at[block], g_send.at[s], g_recv.at[s], peer(s))

    for s in range(1, NUM_DEV):
        gram_copy(s, me).start()
    for s in range(1, NUM_DEV):
        gram_copy(s, me).wait_recv()
    gram_sum = gram[0]
    for d in range(1, NUM_DEV):
        gram_sum = gram_sum + gram[d]
    m = {}
    for k, (t, u) in enumerate(PAIRS):
        m[t, u] = m[u, t] = gram_sum[k:k + 1, :]
    step_scale = (m[0, 0] + m[1, 1] + m[2, 2] + m[3, 3]) / TASKS
    al = [jnp.full((1, 128), 1.0 / TASKS, F32) for _ in range(TASKS)]
    for _ in range(SOLVER_STEPS):
        raised = []
        for t in range(TASKS):
            pull = (m[t, 0] * al[0] + m[t, 1] * al[1]) + (m[t, 2] * al[2] + m[t, 3] * al[3])
            raised.append(al[t] * jnp.exp(-pull / step_scale))
        norm = (raised[0] + raised[1]) + (raised[2] + raised[3])
        al = [r / norm for r in raised]
    for t in range(TASKS):
        alpha_ref[t] = jnp.max(al[t])

    for c in range(DIM // 128):
        cols = slice(128 * c, 128 * c + 128)
        comb = al[0] * acc1[0, :, cols]
        for t in range(1, TASKS):
            comb = comb + al[t] * acc1[t, :, cols]
        gsend[cols, :] = comb.T

    def o_copy(s):
        dev = peer(s)
        rows = pl.ds(pl.multiple_of(dev * FEAT, FEAT), FEAT)
        return remote(gsend.at[rows, :], grecv.at[s], o_send.at[s], o_recv.at[s], dev)

    order = (6, 7, 4, 5, 2, 3, 1)
    for s in order:
        o_copy(s).start()

    for c in range(DIM // 128):
        cols = slice(128 * c, 128 * c + 128)
        comb = al[0] * acc2[0, :, cols]
        for t in range(1, TASKS):
            comb = comb + al[t] * acc2[t, :, cols]
        stage2[pl.ds(c, HID, stride=DIM // 128), :] = comb
    store2 = local(stage2, out2_hbm, 0)
    store2.start()

    per = HID // 128

    def place(dev, block):
        for b in range(per):
            stage1[pl.ds(dev * per + b, FEAT, stride=HIDDEN // 128), :] = block[:, 128 * b:128 * b + 128]

    def owner(slot):
        hop = slot // 2
        first, second = (1 if hop in (1, 3) else 0), (1 if hop in (2, 3) else 0)
        oc = flip(core, jnp.int32(slot % 2))
        bx = first * (1 - oc) + second * oc
        by = first * oc + second * (1 - oc)
        return flip(cx, bx) * 2 + flip(cy, by) * 4 + oc

    place(me, gsend[pl.ds(pl.multiple_of(me * FEAT, FEAT), FEAT), :])
    for s in (1, 2, 3, 4, 5, 6, 7):
        o_copy(s).wait_recv()
        place(owner(s), grecv[s])
    store1 = local(stage1, out1_hbm, 1)
    store1.start()

    x_copy(0, 1).wait_send()
    for k in (4, 3, 5, 6, 7):
        x_copy(0, k).wait_send()
    for s in range(1, NUM_DEV):
        e_copy(s).wait_send()
        c_copy(s).wait_send()
        gram_copy(s, me).wait_send()
        o_copy(s).wait_send()
    store2.wait()
    store1.wait()


def solution(mesh):
    def local_step(x_loc, w_in, w_out, heads, lab_loc, mask_loc):
        head_rows = jnp.pad(heads.transpose(2, 0, 1), ((0, 1), (0, 8 - TASKS), (0, 0))).reshape(HEAD_ROWS, DIM)
        hbm = pl.BlockSpec(memory_space=pl.ANY)
        vmem = pl.BlockSpec(memory_space=pltpu.VMEM)
        sem = pltpu.SemaphoreType.DMA((NUM_DEV,))
        v = pltpu.VMEM
        flat = NUM_DEV * 0 + DIM * HIDDEN // NUM_DEV // 128
        alpha, out1, out2 = pl.pallas_call(
            kernel,
            out_shape=(
                jax.ShapeDtypeStruct((TASKS,), F32),
                jax.ShapeDtypeStruct((flat, 128), F32),
                jax.ShapeDtypeStruct((flat, 128), F32),
            ),
            in_specs=[hbm, hbm, hbm, vmem, vmem, vmem],
            out_specs=(pl.BlockSpec(memory_space=pltpu.SMEM), hbm, hbm),
            scratch_shapes=[
                v((NUM_DEV, TOK, DIM), BF16),
                v((HIDDEN // CHUNK, DIM, CHUNK), BF16),
                v((HIDDEN // CHUNK, CHUNK, DIM), BF16),
                v((DIM, HID), BF16),
                v((HID, DIM), BF16),
                v((HID, DIM), BF16),
                v((ROWS, CHUNK), BF16),
                v((TOK, DIM), F32),
                v((HEAD_ROWS, TOK), F32),
                v((NUM_DEV, HEAD_ROWS, TOK), BF16),
                v((TOK, HEAD_ROWS), BF16),
                v((TASKS, HEAD_ROWS, DIM), BF16),
                v((HID, TOK), BF16),
                v((HID, TOK), F32),
                v((TOK, DIM), BF16),
                v((HID, TOK), BF16),
                v((TASKS, HID, DIM), F32),
                v((TASKS, HID, DIM), F32),
                v((NUM_DEV, 8, 128), F32),
                v((8, DIM), F32),
                v((NUM_DEV, 16, 128), F32),
                v((DIM, HID), F32),
                v((NUM_DEV, FEAT, HID), F32),
                v((flat, 128), F32),
                v((flat, 128), F32),
                sem, sem, sem, sem, sem, sem, sem, sem, sem, sem,
                pltpu.SemaphoreType.DMA((3 + 2 * (HIDDEN // CHUNK),)),
            ],
            compiler_params=pltpu.CompilerParams(collective_id=0, has_side_effects=True, vmem_limit_bytes=66_000_000),
            name="trunk",
        )(x_loc, w_in, w_out, head_rows, lab_loc, mask_loc)
        return alpha, out1.reshape(-1), out2.reshape(-1)

    return jax.shard_map(local_step, mesh=mesh, in_specs=(P("data", None), P(), P(), P(), P(None, "data"), P(None, "data")), out_specs=(P(), P("data"), P("data")), check_vma=False)
```

time: 898 us -> 149 us (0.17)
  waiting for transfers between devices: 351 us -> 0 us
  local copies, waits for them, and re-layouts: 208 us -> 6.09 us
  matrix products: 169 us -> 0 us
  Pallas kernels: 0 us -> 142 us
  other arithmetic: 106 us -> 0 us
  blocking collectives: 47.6 us -> 0 us
  starting transfers between devices: 9.27 us -> 0 us
    all_to_all x2 -> x0, waiting for transfers between devices: 351 us -> none  [local_step(): arrived = lax.all_to_all(scaled, 'data', 1, 1, tiled=True)]
    dot_general x8 -> x0, matrix products: 169 us -> none  [the longest x2 49.4 us: gram_of(): jnp.einsum('tk,sk->ts', grad_rows, grad_rows, precision=lax.Precision.HIG...]
    pallas_call x0 -> x1, Pallas kernels: none -> 142 us  [local_step(): pl.pallas_call(kernel, out_shape=(jax.ShapeDtypeStruct((TASKS,), F32), ja...]
    transpose x2 -> x0, local copies, waits for them, and re-layouts: 73.5 us -> none  [the longest x1 36.8 us: device_grads(): jnp.einsum('bd,tbf->tdf', x_loc, d_pre, preferred_element_type=jnp.float32)]
    reshape x2 -> x1, local copies, waits for them, and re-layouts: 71.7 us -> 1.35 us  [local_step(): jnp.pad(heads.transpose(2, 0, 1), ((0, 1), (0, 8 - TASKS), (0, 0)))]
    reduce_sum x46 -> x0, other arithmetic: 61.8 us -> none  [the longest x2 25.8 us: local_step(): shards.append(arrived.sum(axis=1, dtype=jnp.float32))]
    convert_element_type x2 -> x0, local copies, waits for them, and re-layouts: 60.2 us -> none  [local_step(): (grad_full.reshape(num_tasks, group_size, -1) * inv_count[:, None, None])...]
    psum x2 -> x0, blocking collectives: 47.6 us -> none  [the longest x1 25.2 us: local_step(): label_count = lax.psum(mask_loc.sum(axis=1), 'data')]
  transfers between devices with their start and end apart: 2 -> 0, of which waited for: 2 -> 0; matrix products, arithmetic and copies ran while one was open for 7% -> 0% of each run, Pallas kernels for 0% -> 0%
where the time goes in v1:
time: 149 us
  Pallas kernels  142 us (95%)
  local copies, waits for them, and re-layouts  6.09 us (4%)
    pallas_call x1, Pallas kernels, local_step(): pl.pallas_call(kernel, out_shape=(jax.ShapeDtypeStruct((TASKS,), F32), ja...  142 us
    unnamed x5, local copies, waits for them, and re-layouts  4.74 us

profile of v1, /device:TPU:0, one launch (start us, length us, event | category | flops | bytes accessed | tf_op | source)
XLA Modules:
  0.0 148.7 jit_solution(10360892750043834656)
XLA Ops:
  0.6 1.4 pad_bitcast_fusion.head_ref
  2.0 142.0 %trunk.1 = (f32[4]{0:T(128)}, f32[2304,128]{1,0:T(8,128)}, f32[2304,128]{1,0:T(8,128)}) custom-call(bf16[1024,768]{1,0:T(8,128)(2,1)} %x_hbm.1, bf16[768,3072]{1,0:T(8,128)(2,1)} %w_in_hbm.1, bf16[3072,768]{1,0:T(8,128)(2,1)} %w_out_hbm.1, bf16[32,768]{1,0:T(8,128)(2,1)} %pad_bitcast_fusion.head_ref, s32[4,1024]{1,0:T(4,128)} %lab_ref.1, s32[4,1024]{1,0:T(4,128)} %mask_ref.1), custom_call_target="tpu_custom_call" | custom-call | tf_op jit(solution)/shard_map/trunk/pallas_call | solution.py:304
  144.0 1.2 copy.12
  145.2 0.0 copy-start
  145.2 2.5 %copy.13 = f32[294912]{0:T(1024)} copy(f32[294912]{0:T(1024)} %bitcast.6) | data formatting | bytes 2359296
  147.6 0.0 copy-done
  147.6 1.1 copy.14
Async XLA Ops:
  145.2 2.5 %copy-start = (f32[2304,128]{1,0:T(8,128)S(1)}, f32[2304,128]{1,0:T(8,128)}, u32[]{:S(2)}) copy-start(f32[2304,128]{1,0:T(8,128)} %get-tuple-element.8) | copy-start | bytes 3538948

commit v2 on v1

--- a/solution.py
+++ b/solution.py
@@ -19,6 +19,8 @@
 HEAD_ROWS = 32
 CHUNK = 768
 ROWS = 512
+NCHUNK = HIDDEN // CHUNK
+QUARTER = TOK // TASKS
 PAIRS = [(t, s) for t in range(TASKS) for s in range(t, TASKS)]
 GELU_C = 0.7978845608028654
 GELU_K = 0.044715
@@ -36,21 +38,25 @@
     return jnp.concatenate([row] * (width // row.shape[1]), axis=1)
 
 
+def gelu_parts(p):
+    a = (GELU_C * GELU_K) * (p * p)
+    th = jnp.tanh(p * (a + GELU_C))
+    return a, th, 0.5 + 0.5 * th
+
+
 def gelu_value(p):
-    return p * (0.5 * (1.0 + jnp.tanh(GELU_C * (p + GELU_K * (p * p * p)))))
+    return p * gelu_parts(p)[2]
 
 
 def gelu_both(p):
-    sq = p * p
-    th = jnp.tanh(GELU_C * (p + GELU_K * (sq * p)))
-    cdf = 0.5 * (1.0 + th)
-    slope = cdf + (0.5 * p) * ((1.0 - th * th) * (GELU_C * (1.0 + (3.0 * GELU_K) * sq)))
+    a, th, cdf = gelu_parts(p)
+    slope = cdf + ((1.0 - th * th) * p) * (1.5 * a + 0.5 * GELU_C)
     return p * cdf, slope
 
 
 def kernel(x_hbm, w_in_hbm, w_out_hbm, head_ref, lab_ref, mask_ref, alpha_ref, out1_hbm, out2_hbm,
-           xs, w1, w2, w1j, w1t, w2j, abuf, zacc, ef, es, etok, hm, act_t, slope_t, dz, q_t, acc1, acc2,
-           cnt, inv, gram, gsend, grecv, stage1, stage2,
+           xs, w1, w2, w1j, w1t, w2j, abuf0, abuf1, zacc, hrow, hbc, ef, es, ecur, act0, act1, slope0, slope1,
+           dz0, dz1, q0, q1, acc1, acc2, cnt, inv, gram, gsend, grecv, stage1, stage2,
            x_send, x_recv, e_send, e_recv, c_send, c_recv, g_send, g_recv, o_send, o_recv, l_sem):
     me = lax.axis_index("data")
     core = lax.rem(me, 2)
@@ -84,55 +90,79 @@
     def local(src, dst, i):
         return pltpu.make_async_copy(src, dst, l_sem.at[i])
 
-    nchunk = HIDDEN // CHUNK
+    def load_w1(i):
+        return local(w_in_hbm.at[:, pl.ds(pl.multiple_of(CHUNK * i, CHUNK), CHUNK)], w1.at[i], 3 + i)
+
+    def load_w2(i):
+        return local(w_out_hbm.at[pl.ds(pl.multiple_of(CHUNK * i, CHUNK), CHUNK), :], w2.at[i], 3 + NCHUNK + i)
+
     load_x = local(x_hbm, xs.at[0], 0)
-    load_w1 = [local(w_in_hbm.at[:, pl.ds(CHUNK * i, CHUNK)], w1.at[i], 1 + i) for i in range(nchunk)]
-    load_w2 = [local(w_out_hbm.at[pl.ds(CHUNK * i, CHUNK), :], w2.at[i], 1 + nchunk + i) for i in range(nchunk)]
-    load_w1j = local(w_in_hbm.at[:, pl.ds(pl.multiple_of(me * HID, HID), HID)], w1j, 1 + 2 * nchunk)
-    load_w2j = local(w_out_hbm.at[pl.ds(pl.multiple_of(me * HID, HID), HID), :], w2j, 2 + 2 * nchunk)
+    load_w1j = local(w_in_hbm.at[:, pl.ds(pl.multiple_of(me * HID, HID), HID)], w1j, 1)
+    load_w2j = local(w_out_hbm.at[pl.ds(pl.multiple_of(me * HID, HID), HID), :], w2j, 2)
     load_x.start()
-    for i in range(nchunk):
-        load_w1[i].start()
-        load_w2[i].start()
     load_w1j.start()
+    for i in range(NCHUNK):
+        load_w1(i).start()
+        load_w2(i).start()
     load_w2j.start()
+
+    barrier = pltpu.get_barrier_semaphore()
+    for s in range(1, NUM_DEV):
+        pl.semaphore_signal(barrier, inc=1, device_id=(peer(s),), device_id_type=MESH)
 
     counts = jnp.sum(mask_ref[...].astype(F32), axis=1, keepdims=True)
     cnt[0, 0:TASKS, :] = jnp.broadcast_to(counts, (TASKS, 128))
     cnt[0, TASKS:8, :] = jnp.zeros((8 - TASKS, 128), F32)
-    head = head_ref[...].astype(F32)
-    row_task = lax.rem(lax.broadcasted_iota(jnp.int32, (HEAD_ROWS, DIM), 0), 8)
-    for t in range(TASKS):
-        hm[t] = jnp.where(row_task == t, head, 0.0).astype(BF16)
-
-    barrier = pltpu.get_barrier_semaphore()
-    for s in range(1, NUM_DEV):
-        pl.semaphore_signal(barrier, inc=1, device_id=(peer(s),), device_id_type=MESH)
+    hrow[...] = jnp.zeros_like(hrow)
+    for c in range(CLASSES):
+        hrow[8 * c:8 * c + TASKS, :] = head_ref[c].astype(F32)
+    head = hrow[...].astype(BF16)
+
     pl.semaphore_wait(barrier, NUM_DEV - 1)
-
     load_x.wait()
     x_copy(0, 1).start()
     x_copy(0, 2).start()
     for s in range(1, NUM_DEV):
         c_copy(s).start()
 
+    block = lax.div(lax.broadcasted_iota(jnp.int32, (HEAD_ROWS, TASKS * CLASSES * 128), 1), 128)
+    pick = lax.rem(block, CLASSES) * 8 + lax.div(block, CLASSES)
+    ones = (lax.broadcasted_iota(jnp.int32, block.shape, 0) == pick).astype(F32).astype(BF16)
+    wide = dot_nn(hrow[...].T.astype(BF16), ones)
+    for k in range(TASKS * CLASSES):
+        hbc[k] = wide[:, 128 * k:128 * k + 128]
+    load_w1j.wait()
+    w1t[...] = w1j[...].astype(F32).T.astype(BF16)
+
+    abuf1[...] = jnp.zeros_like(abuf1)
     zacc[...] = xs[0].astype(F32)
-    for c in load_w1 + load_w2:
-        c.wait()
-
-    def forward(i, carry):
-        h = lax.div(i, TOK // ROWS)
-        r = pl.ds(pl.multiple_of(lax.rem(i, TOK // ROWS) * ROWS, ROWS), ROWS)
-        abuf[...] = gelu_value(dot_nn(xs[0, r, :], w1[h])).astype(BF16)
-        zacc[r, :] += dot_nn(abuf[...], w2[h])
+    half0, half1 = slice(0, ROWS), slice(ROWS, TOK)
+
+    def forward(h, carry):
+        load_w1(h).wait()
+        load_w2(h).wait()
+        acc1[h] = jnp.zeros((HID, DIM), F32)
+        acc2[h] = jnp.zeros((HID, DIM), F32)
+        abuf0[...] = gelu_value(dot_nn(xs[0, half0, :], w1[h])).astype(BF16)
+        zacc[half1, :] += dot_nn(abuf1[...], w2[jnp.maximum(h - 1, 0)])
+        abuf1[...] = gelu_value(dot_nn(xs[0, half1, :], w1[h])).astype(BF16)
+        zacc[half0, :] += dot_nn(abuf0[...], w2[h])
         return carry
 
-    lax.fori_loop(0, nchunk * (TOK // ROWS), forward, 0)
-
-    ef[...] = jnp.zeros_like(ef)
+    lax.fori_loop(0, NCHUNK, forward, 0)
+    zacc[half1, :] += dot_nn(abuf1[...], w2[NCHUNK - 1])
+
+    acts, slopes, dzs, qs = (act0, act1), (slope0, slope1), (dz0, dz1), (q0, q1)
+
+    def preact(slot, part, quarter):
+        r = pl.ds(pl.multiple_of(quarter * QUARTER, QUARTER), QUARTER)
+        a, sl = gelu_both(dot_nt(w1t[...], xs[slot, r, :]))
+        acts[part][:, r] = a.astype(BF16)
+        slopes[part][:, r] = sl
+
     for r in range(TOK // ROWS):
         cols = slice(r * ROWS, (r + 1) * ROWS)
-        logits = dot_nt(head_ref[...], zacc[cols, :].astype(BF16))
+        logits = dot_nt(head, zacc[cols, :].astype(BF16))
         l = [logits[8 * c:8 * c + TASKS] for c in range(CLASSES)]
         top = jnp.maximum(jnp.maximum(l[0], l[1]), l[2])
         ex = [jnp.exp(v - top) for v in l]
@@ -140,60 +170,83 @@
         lab = lab_ref[:, cols]
         m = mask_ref[:, cols].astype(F32)
         for c in range(CLASSES):
-            ef[8 * c:8 * c + TASKS, cols] = m * (ex[c] / total - (lab == c).astype(F32))
+            err = m * (ex[c] / total - (lab == c).astype(F32))
+            for t in range(TASKS):
+                ef[8 * t + c:8 * t + c + 1, cols] = err[t:t + 1]
+    for t in range(TASKS):
+        ef[8 * t + CLASSES:8 * t + 8, :] = jnp.zeros((8 - CLASSES, TOK), F32)
     es[0] = ef[...].astype(BF16)
-
-    acc1[...] = jnp.zeros_like(acc1)
-    acc2[...] = jnp.zeros_like(acc2)
-    load_w1j.wait()
+    for t in range(TASKS):
+        ecur[0, t] = es[0, 8 * t:8 * t + 8, :].astype(F32)
+
+    for k in range(TOK // QUARTER):
+        preact(0, 0, k)
+
+    def make_dz(dst, part, t):
+        e = ecur[part, t]
+        rows = [jnp.broadcast_to(e[c:c + 1, :], (16, TOK)) for c in range(CLASSES)]
+        for k in range(DIM // 16):
+            f = slice(16 * k, 16 * k + 16)
+            h = [lanes(hbc[CLASSES * t + c, f, :], TOK) for c in range(CLASSES)]
+            dst[f, :] = (h[0] * rows[0] + h[1] * rows[1] + h[2] * rows[2]).astype(BF16)
+
+    for s in range(1, NUM_DEV):
+        e_copy(s).start()
+    make_dz(dz0, 0, 0)
     load_w2j.wait()
-    w1t[...] = w1j[...].astype(F32).T.astype(BF16)
-
-    for s in range(1, NUM_DEV):
-        e_copy(s).start()
     total_cnt = cnt[0]
     for s in range(1, NUM_DEV):
         c_copy(s).wait_recv()
         total_cnt = total_cnt + cnt[s]
     inv[...] = lanes(1.0 / jnp.maximum(total_cnt, 1.0), DIM)
 
-    def shard(s, carry):
+    def tokens_ready(s):
         for k in range(1, NUM_DEV):
-            @pl.when(s == k)
+            @pl.when(s == k - 1)
             def _():
                 x_copy(0, k).wait_recv()
-                e_copy(k).wait_recv()
-                if k == 1:
+                if k == 2:
                     x_copy(0, 2).wait_send()
                     x_copy(0, 4).start()
+                    x_copy(2, 6).start()
                 if k in (2, 4, 6):
                     x_copy(k, k + 1).start()
-                if k == 2:
-                    x_copy(2, 6).start()
-
-        etok[...] = es[s].astype(F32).T.astype(BF16)
-
-        def preact(i, c):
-            r = pl.ds(pl.multiple_of(i * ROWS, ROWS), ROWS)
-            a, sl = gelu_both(dot_nt(w1t[...], xs[s, r, :]))
-            act_t[:, r] = a.astype(BF16)
-            slope_t[:, r] = sl
-            return c
-
-        lax.fori_loop(0, TOK // ROWS, preact, 0)
-
-        def task(t, c):
-            scale = inv[pl.ds(t, 1), :]
-            dz[...] = dot_nn(etok[...], hm[t]).astype(BF16)
-            q_t[...] = (dot_nt(w2j[...], dz[...]) * slope_t[...]).astype(BF16)
-            acc2[t] += (dot_nn(act_t[...], dz[...]) * scale).astype(BF16).astype(F32)
-            acc1[t] += (dot_nn(q_t[...], xs[s]) * scale).astype(BF16).astype(F32)
-            return c
-
-        lax.fori_loop(0, TASKS, task, 0)
+
+    def errors_ready(s, part):
+        for k in range(1, NUM_DEV):
+            @pl.when(s == k - 1)
+            def _():
+                e_copy(k).wait_recv()
+                for t in range(TASKS):
+                    ecur[part, t] = es[k, 8 * t:8 * t + 8, :].astype(F32)
+
+    def run_task(s, part, t, j, next_part, next_t):
+        nxt = jnp.minimum(s + 1, NUM_DEV - 1)
+        scale = inv[pl.ds(t, 1), :]
+        qs[j][...] = (dot_nn(w2j[...], dzs[j][...]) * slopes[part][...]).astype(BF16)
+        acc2[t] += (dot_nt(acts[part][...], dzs[j][...]) * scale).astype(BF16).astype(F32)
+        make_dz(dzs[1 - j], next_part, next_t)
+        preact(nxt, 1 - part, t)
+        acc1[t] += (dot_nn(qs[j][...], xs[s]) * scale).astype(BF16).astype(F32)
+
+    def shard_pair(sp, carry):
+        for part in range(2):
+            s = 2 * sp + part
+            tokens_ready(s)
+
+            def task_pair(tp, c):
+                @pl.when(tp == 1)
+                def _():
+                    errors_ready(s, 1 - part)
+                run_task(s, part, 2 * tp, 0, part, 2 * tp + 1)
+                wrap = lax.div(2 * tp + 2, TASKS)
+                run_task(s, part, 2 * tp + 1, 1, part + wrap * (1 - 2 * part), 2 * tp + 2 - TASKS * wrap)
+                return c
+
+            lax.fori_loop(0, TASKS // 2, task_pair, 0)
         return carry
 
-    lax.fori_loop(0, NUM_DEV, shard, 0)
+    lax.fori_loop(0, NUM_DEV // 2, shard_pair, 0)
 
     def gram_rows(i, sums):
         r = pl.ds(pl.multiple_of(i * 8, 8), 8)
@@ -295,12 +348,11 @@
 
 def solution(mesh):
     def local_step(x_loc, w_in, w_out, heads, lab_loc, mask_loc):
-        head_rows = jnp.pad(heads.transpose(2, 0, 1), ((0, 1), (0, 8 - TASKS), (0, 0))).reshape(HEAD_ROWS, DIM)
         hbm = pl.BlockSpec(memory_space=pl.ANY)
         vmem = pl.BlockSpec(memory_space=pltpu.VMEM)
         sem = pltpu.SemaphoreType.DMA((NUM_DEV,))
         v = pltpu.VMEM
-        flat = NUM_DEV * 0 + DIM * HIDDEN // NUM_DEV // 128
+        flat = DIM * HIDDEN // NUM_DEV // 128
         alpha, out1, out2 = pl.pallas_call(
             kernel,
             out_shape=(
@@ -312,20 +364,26 @@
             out_specs=(pl.BlockSpec(memory_space=pltpu.SMEM), hbm, hbm),
             scratch_shapes=[
                 v((NUM_DEV, TOK, DIM), BF16),
-                v((HIDDEN // CHUNK, DIM, CHUNK), BF16),
-                v((HIDDEN // CHUNK, CHUNK, DIM), BF16),
+                v((NCHUNK, DIM, CHUNK), BF16),
+                v((NCHUNK, CHUNK, DIM), BF16),
                 v((DIM, HID), BF16),
                 v((HID, DIM), BF16),
                 v((HID, DIM), BF16),
                 v((ROWS, CHUNK), BF16),
+                v((ROWS, CHUNK), BF16),
                 v((TOK, DIM), F32),
+                v((HEAD_ROWS, DIM), F32),
+                v((TASKS * CLASSES, DIM, 128), F32),
                 v((HEAD_ROWS, TOK), F32),
                 v((NUM_DEV, HEAD_ROWS, TOK), BF16),
-                v((TOK, HEAD_ROWS), BF16),
-                v((TASKS, HEAD_ROWS, DIM), BF16),
+                v((2, TASKS, 8, TOK), F32),
+                v((HID, TOK), BF16),
                 v((HID, TOK), BF16),
                 v((HID, TOK), F32),
-                v((TOK, DIM), BF16),
+                v((HID, TOK), F32),
+                v((DIM, TOK), BF16),
+                v((DIM, TOK), BF16),
+                v((HID, TOK), BF16),
                 v((HID, TOK), BF16),
                 v((TASKS, HID, DIM), F32),
                 v((TASKS, HID, DIM), F32),
@@ -337,11 +395,11 @@
                 v((flat, 128), F32),
                 v((flat, 128), F32),
                 sem, sem, sem, sem, sem, sem, sem, sem, sem, sem,
-                pltpu.SemaphoreType.DMA((3 + 2 * (HIDDEN // CHUNK),)),
+                pltpu.SemaphoreType.DMA((3 + 2 * NCHUNK,)),
             ],
             compiler_params=pltpu.CompilerParams(collective_id=0, has_side_effects=True, vmem_limit_bytes=66_000_000),
             name="trunk",
-        )(x_loc, w_in, w_out, head_rows, lab_loc, mask_loc)
+        )(x_loc, w_in, w_out, heads.transpose(2, 0, 1), lab_loc, mask_loc)
         return alpha, out1.reshape(-1), out2.reshape(-1)
 
     return jax.shard_map(local_step, mesh=mesh, in_specs=(P("data", None), P(), P(), P(), P(None, "data"), P(None, "data")), out_specs=(P(), P("data"), P("data")), check_vma=False)

time: 149 us -> 130 us (0.87)
  Pallas kernels: 142 us -> 124 us
    pallas_call x1, Pallas kernels: 142 us -> 124 us  [local_step(): pl.pallas_call(kernel, out_shape=(jax.ShapeDtypeStruct((TASKS,), F32), ja...]
where the time goes in v2:
time: 130 us; the launch traced here: 129 us
  Pallas kernels  124 us (95%)
  local copies, waits for them, and re-layouts  4.74 us (4%)
    pallas_call x1, Pallas kernels, local_step(): pl.pallas_call(kernel, out_shape=(jax.ShapeDtypeStruct((TASKS,), F32), ja...  124 us
    unnamed x5, local copies, waits for them, and re-layouts  4.74 us

profile of v2, /device:TPU:0, one launch (start us, length us, event | category | flops | bytes accessed | tf_op | source)
XLA Modules:
  0.0 129.5 jit_solution(11704095177163046329)
XLA Ops:
  0.6 124.1 %trunk.1 = (f32[4]{0:T(128)}, f32[2304,128]{1,0:T(8,128)}, f32[2304,128]{1,0:T(8,128)}) custom-call(bf16[1024,768]{1,0:T(8,128)(2,1)} %x_hbm.1, bf16[768,3072]{1,0:T(8,128)(2,1)} %w_in_hbm.1, bf16[3072,768]{1,0:T(8,128)(2,1)} %w_out_hbm.1, bf16[3,4,768]{2,1,0:T(4,128)(2,1)} %bitcast.5, s32[4,1024]{1,0:T(4,128)} %lab_ref.1, s32[4,1024]{1,0:T(4,128)} %mask_ref.1), custom_call_target="tpu_custom_call" | custom-call | tf_op jit(solution)/shard_map/trunk/pallas_call | solution.py:356
  124.8 1.2 copy.12
  125.9 0.0 copy-start
  125.9 2.5 %copy.13 = f32[294912]{0:T(1024)} copy(f32[294912]{0:T(1024)} %bitcast.4) | data formatting | bytes 2359296
  128.4 0.0 copy-done
  128.4 1.1 copy.14
Async XLA Ops:
  125.9 2.5 %copy-start = (f32[2304,128]{1,0:T(8,128)S(1)}, f32[2304,128]{1,0:T(8,128)}, u32[]{:S(2)}) copy-start(f32[2304,128]{1,0:T(8,128)} %get-tuple-element.8) | copy-start | bytes 3538948

commit v3 on v2

--- a/solution.py
+++ b/solution.py
@@ -199,6 +199,8 @@
         c_copy(s).wait_recv()
         total_cnt = total_cnt + cnt[s]
     inv[...] = lanes(1.0 / jnp.maximum(total_cnt, 1.0), DIM)
+    x_copy(0, 2).wait_send()
+    x_copy(0, 4).start()
 
     def tokens_ready(s):
         for k in range(1, NUM_DEV):
@@ -206,8 +208,6 @@
             def _():
                 x_copy(0, k).wait_recv()
                 if k == 2:
-                    x_copy(0, 2).wait_send()
-                    x_copy(0, 4).start()
                     x_copy(2, 6).start()
                 if k in (2, 4, 6):
                     x_copy(k, k + 1).start()

time: 130 us -> 128 us (0.985)
  Pallas kernels: 124 us -> 122 us
    pallas_call x1, Pallas kernels: 124 us -> 122 us  [local_step(): pl.pallas_call(kernel, out_shape=(jax.ShapeDtypeStruct((TASKS,), F32), ja...]
where the time goes in v3:
time: 128 us
  Pallas kernels  122 us (95%)
  local copies, waits for them, and re-layouts  4.74 us (4%)
    pallas_call x1, Pallas kernels, local_step(): pl.pallas_call(kernel, out_shape=(jax.ShapeDtypeStruct((TASKS,), F32), ja...  122 us
    unnamed x5, local copies, waits for them, and re-layouts  4.74 us

profile of v3, /device:TPU:0, one launch (start us, length us, event | category | flops | bytes accessed | tf_op | source)
XLA Modules:
  0.0 127.8 jit_solution(10048582876024354793)
XLA Ops:
  0.6 122.4 %trunk.1 = (f32[4]{0:T(128)}, f32[2304,128]{1,0:T(8,128)}, f32[2304,128]{1,0:T(8,128)}) custom-call(bf16[1024,768]{1,0:T(8,128)(2,1)} %x_hbm.1, bf16[768,3072]{1,0:T(8,128)(2,1)} %w_in_hbm.1, bf16[3072,768]{1,0:T(8,128)(2,1)} %w_out_hbm.1, bf16[3,4,768]{2,1,0:T(4,128)(2,1)} %bitcast.5, s32[4,1024]{1,0:T(4,128)} %lab_ref.1, s32[4,1024]{1,0:T(4,128)} %mask_ref.1), custom_call_target="tpu_custom_call" | custom-call | tf_op jit(solution)/shard_map/trunk/pallas_call | solution.py:356
  123.1 1.2 copy.12
  124.2 0.0 copy-start
  124.3 2.5 %copy.13 = f32[294912]{0:T(1024)} copy(f32[294912]{0:T(1024)} %bitcast.4) | data formatting | bytes 2359296
  126.7 0.0 copy-done
  126.7 1.1 copy.14
Async XLA Ops:
  124.2 2.5 %copy-start = (f32[2304,128]{1,0:T(8,128)S(1)}, f32[2304,128]{1,0:T(8,128)}, u32[]{:S(2)}) copy-start(f32[2304,128]{1,0:T(8,128)} %get-tuple-element.8) | copy-start | bytes 3538948

commit v4 on v3

--- a/solution.py
+++ b/solution.py
@@ -54,9 +54,9 @@
     return p * cdf, slope
 
 
-def kernel(x_hbm, w_in_hbm, w_out_hbm, head_ref, lab_ref, mask_ref, alpha_ref, out1_hbm, out2_hbm,
+def kernel(x_hbm, w_in_hbm, w_out_hbm, head_ref, lab_ref, mask_ref, alpha_ref, gx_hbm, out2_hbm,
            xs, w1, w2, w1j, w1t, w2j, abuf0, abuf1, zacc, hrow, hbc, ef, es, ecur, act0, act1, slope0, slope1,
-           dz0, dz1, q0, q1, acc1, acc2, cnt, inv, gram, gsend, grecv, stage1, stage2,
+           dz0, dz1, q0, q1, acc1, acc2, cnt, inv, gram, gsend, stage2,
            x_send, x_recv, e_send, e_recv, c_send, c_recv, g_send, g_recv, o_send, o_recv, l_sem):
     me = lax.axis_index("data")
     core = lax.rem(me, 2)
@@ -138,6 +138,14 @@
     zacc[...] = xs[0].astype(F32)
     half0, half1 = slice(0, ROWS), slice(ROWS, TOK)
 
+    acts, slopes, dzs, qs = (act0, act1), (slope0, slope1), (dz0, dz1), (q0, q1)
+
+    def preact(slot, part, quarter):
+        r = pl.ds(pl.multiple_of(quarter * QUARTER, QUARTER), QUARTER)
+        a, sl = gelu_both(dot_nt(w1t[...], xs[slot, r, :]))
+        acts[part][:, r] = a.astype(BF16)
+        slopes[part][:, r] = sl
+
     def forward(h, carry):
         load_w1(h).wait()
         load_w2(h).wait()
@@ -147,18 +155,11 @@
         zacc[half1, :] += dot_nn(abuf1[...], w2[jnp.maximum(h - 1, 0)])
         abuf1[...] = gelu_value(dot_nn(xs[0, half1, :], w1[h])).astype(BF16)
         zacc[half0, :] += dot_nn(abuf0[...], w2[h])
+        preact(0, 0, h)
         return carry
 
     lax.fori_loop(0, NCHUNK, forward, 0)
     zacc[half1, :] += dot_nn(abuf1[...], w2[NCHUNK - 1])
-
-    acts, slopes, dzs, qs = (act0, act1), (slope0, slope1), (dz0, dz1), (q0, q1)
-
-    def preact(slot, part, quarter):
-        r = pl.ds(pl.multiple_of(quarter * QUARTER, QUARTER), QUARTER)
-        a, sl = gelu_both(dot_nt(w1t[...], xs[slot, r, :]))
-        acts[part][:, r] = a.astype(BF16)
-        slopes[part][:, r] = sl
 
     for r in range(TOK // ROWS):
         cols = slice(r * ROWS, (r + 1) * ROWS)
@@ -179,14 +180,11 @@
     for t in range(TASKS):
         ecur[0, t] = es[0, 8 * t:8 * t + 8, :].astype(F32)
 
-    for k in range(TOK // QUARTER):
-        preact(0, 0, k)
-
     def make_dz(dst, part, t):
         e = ecur[part, t]
-        rows = [jnp.broadcast_to(e[c:c + 1, :], (16, TOK)) for c in range(CLASSES)]
-        for k in range(DIM // 16):
-            f = slice(16 * k, 16 * k + 16)
+        rows = [jnp.broadcast_to(e[c:c + 1, :], (8, TOK)) for c in range(CLASSES)]
+        for k in range(DIM // 8):
+            f = slice(8 * k, 8 * k + 8)
             h = [lanes(hbc[CLASSES * t + c, f, :], TOK) for c in range(CLASSES)]
             dst[f, :] = (h[0] * rows[0] + h[1] * rows[1] + h[2] * rows[2]).astype(BF16)
 
@@ -298,7 +296,7 @@
     def o_copy(s):
         dev = peer(s)
         rows = pl.ds(pl.multiple_of(dev * FEAT, FEAT), FEAT)
-        return remote(gsend.at[rows, :], grecv.at[s], o_send.at[s], o_recv.at[s], dev)
+        return remote(gsend.at[rows, :], gx_hbm.at[me], o_send.at[s], o_recv.at[s], dev)
 
     order = (6, 7, 4, 5, 2, 3, 1)
     for s in order:
@@ -313,26 +311,10 @@
     store2 = local(stage2, out2_hbm, 0)
     store2.start()
 
-    per = HID // 128
-
-    def place(dev, block):
-        for b in range(per):
-            stage1[pl.ds(dev * per + b, FEAT, stride=HIDDEN // 128), :] = block[:, 128 * b:128 * b + 128]
-
-    def owner(slot):
-        hop = slot // 2
-        first, second = (1 if hop in (1, 3) else 0), (1 if hop in (2, 3) else 0)
-        oc = flip(core, jnp.int32(slot % 2))
-        bx = first * (1 - oc) + second * oc
-        by = first * oc + second * (1 - oc)
-        return flip(cx, bx) * 2 + flip(cy, by) * 4 + oc
-
-    place(me, gsend[pl.ds(pl.multiple_of(me * FEAT, FEAT), FEAT), :])
-    for s in (1, 2, 3, 4, 5, 6, 7):
+    keep = local(gsend.at[pl.ds(pl.multiple_of(me * FEAT, FEAT), FEAT), :], gx_hbm.at[me], 1)
+    keep.start()
+    for s in range(1, NUM_DEV):
         o_copy(s).wait_recv()
-        place(owner(s), grecv[s])
-    store1 = local(stage1, out1_hbm, 1)
-    store1.start()
 
     x_copy(0, 1).wait_send()
     for k in (4, 3, 5, 6, 7):
@@ -343,7 +325,39 @@
         gram_copy(s, me).wait_send()
         o_copy(s).wait_send()
     store2.wait()
-    store1.wait()
+    keep.wait()
+
+
+PER = HID // 128
+FLAT = DIM * HIDDEN // NUM_DEV // 128
+HALF = FEAT // 2
+
+
+def finish(alpha_in, gx_hbm, g2_hbm, alpha_ref, out1_hbm, out2_hbm, blocks, stage1, stage2, in_sem, out_sem):
+    loads = [pltpu.make_async_copy(gx_hbm.at[d], blocks.at[d], in_sem.at[d]) for d in range(NUM_DEV)]
+    load2 = pltpu.make_async_copy(g2_hbm, stage2, in_sem.at[NUM_DEV])
+    for c in loads:
+        c.start()
+    load2.start()
+    for t in range(TASKS):
+        alpha_ref[t] = alpha_in[t]
+    for c in loads:
+        c.wait()
+    stores = []
+    for h in range(2):
+        for d in range(NUM_DEV):
+            for b in range(PER):
+                first = h * HALF * (HIDDEN // 128) + d * PER + b
+                stage1[pl.ds(first, HALF, stride=HIDDEN // 128), :] = blocks[d, h * HALF:h * HALF + HALF, 128 * b:128 * b + 128]
+        rows = pl.ds(h * FLAT // 2, FLAT // 2)
+        stores.append(pltpu.make_async_copy(stage1.at[rows, :], out1_hbm.at[rows, :], out_sem.at[h]))
+        stores[-1].start()
+        if h == 0:
+            load2.wait()
+            stores.append(pltpu.make_async_copy(stage2, out2_hbm, out_sem.at[2]))
+            stores[-1].start()
+    for c in stores:
+        c.wait()
 
 
 def solution(mesh):
@@ -352,13 +366,12 @@
         vmem = pl.BlockSpec(memory_space=pltpu.VMEM)
         sem = pltpu.SemaphoreType.DMA((NUM_DEV,))
         v = pltpu.VMEM
-        flat = DIM * HIDDEN // NUM_DEV // 128
-        alpha, out1, out2 = pl.pallas_call(
+        alpha, gx, g2 = pl.pallas_call(
             kernel,
             out_shape=(
                 jax.ShapeDtypeStruct((TASKS,), F32),
-                jax.ShapeDtypeStruct((flat, 128), F32),
-                jax.ShapeDtypeStruct((flat, 128), F32),
+                jax.ShapeDtypeStruct((NUM_DEV, FEAT, HID), F32),
+                jax.ShapeDtypeStruct((FLAT, 128), F32),
             ),
             in_specs=[hbm, hbm, hbm, vmem, vmem, vmem],
             out_specs=(pl.BlockSpec(memory_space=pltpu.SMEM), hbm, hbm),
@@ -391,15 +404,32 @@
                 v((8, DIM), F32),
                 v((NUM_DEV, 16, 128), F32),
                 v((DIM, HID), F32),
-                v((NUM_DEV, FEAT, HID), F32),
-                v((flat, 128), F32),
-                v((flat, 128), F32),
+                v((FLAT, 128), F32),
                 sem, sem, sem, sem, sem, sem, sem, sem, sem, sem,
                 pltpu.SemaphoreType.DMA((3 + 2 * NCHUNK,)),
             ],
             compiler_params=pltpu.CompilerParams(collective_id=0, has_side_effects=True, vmem_limit_bytes=66_000_000),
             name="trunk",
         )(x_loc, w_in, w_out, heads.transpose(2, 0, 1), lab_loc, mask_loc)
+        smem = pl.BlockSpec(memory_space=pltpu.SMEM)
+        alpha, out1, out2 = pl.pallas_call(
+            finish,
+            out_shape=(
+                jax.ShapeDtypeStruct((TASKS,), F32),
+                jax.ShapeDtypeStruct((FLAT, 128), F32),
+                jax.ShapeDtypeStruct((FLAT, 128), F32),
+            ),
+            in_specs=[smem, hbm, hbm],
+            out_specs=(smem, hbm, hbm),
+            scratch_shapes=[
+                v((NUM_DEV, FEAT, HID), F32),
+                v((FLAT, 128), F32),
+                v((FLAT, 128), F32),
+                pltpu.SemaphoreType.DMA((NUM_DEV + 1,)),
+                pltpu.SemaphoreType.DMA((3,)),
+            ],
+            name="finish",
+        )(alpha, gx, g2)
         return alpha, out1.reshape(-1), out2.reshape(-1)
 
     return jax.shard_map(local_step, mesh=mesh, in_specs=(P("data", None), P(), P(), P(), P(None, "data"), P(None, "data")), out_specs=(P(), P("data"), P("data")), check_vma=False)

time: 128 us -> 127 us (level)
  local copies, waits for them, and re-layouts: 4.74 us -> 0 us
  Pallas kernels: 122 us -> 126 us
    unnamed x5 -> x0, local copies, waits for them, and re-layouts: 4.74 us -> none
    pallas_call x0 -> x1, Pallas kernels: none -> 4.24 us  [local_step(): pl.pallas_call(finish, out_shape=(jax.ShapeDtypeStruct((TASKS,), F32), ja...]
where the time goes in v4:
time: 127 us
  Pallas kernels  126 us (99%)
    pallas_call x1, Pallas kernels, local_step(): pl.pallas_call(kernel, out_shape=(jax.ShapeDtypeStruct((TASKS,), F32), ja...  122 us
    pallas_call x1, Pallas kernels, local_step(): pl.pallas_call(finish, out_shape=(jax.ShapeDtypeStruct((TASKS,), F32), ja...  4.24 us

profile of v4, /device:TPU:0, one launch (start us, length us, event | category | flops | bytes accessed | tf_op | source)
XLA Modules:
  0.0 126.6 jit_solution(581721633689381358)
XLA Ops:
  0.6 121.6 %trunk.1 = (f32[4]{0:T(128)}, f32[8,96,384]{2,1,0:T(8,128)}, f32[2304,128]{1,0:T(8,128)}) custom-call(bf16[1024,768]{1,0:T(8,128)(2,1)} %x_hbm.1, bf16[768,3072]{1,0:T(8,128)(2,1)} %w_in_hbm.1, bf16[3072,768]{1,0:T(8,128)(2,1)} %w_out_hbm.1, bf16[3,4,768]{2,1,0:T(4,128)(2,1)} %bitcast.3, s32[4,1024]{1,0:T(4,128)} %lab_ref.1, s32[4,1024]{1,0:T(4,128)} %mask_ref.1), custom_call_target="tpu_custom_call" | custom-call | tf_op jit(solution)/shard_map/trunk/pallas_call | solution.py:369
  122.2 4.2 %finish.1 = (f32[4]{0:T(128)}, f32[2304,128]{1,0:T(8,128)}, f32[2304,128]{1,0:T(8,128)}) custom-call(f32[4]{0:T(128)} %get-tuple-element.9.alpha_in, f32[8,96,384]{2,1,0:T(8,128)} %get-tuple-element.10.gx_hbm, f32[2304,128]{1,0:T(8,128)} %get-tuple-element.11.g2_hbm), custom_call_target="tpu_custom_call" | custom-call | tf_op jit(solution)/shard_map/finish/pallas_call | solution.py:415

commit v5 on v4

--- a/solution.py
+++ b/solution.py
@@ -101,10 +101,8 @@
     load_w2j = local(w_out_hbm.at[pl.ds(pl.multiple_of(me * HID, HID), HID), :], w2j, 2)
     load_x.start()
     load_w1j.start()
-    for i in range(NCHUNK):
-        load_w1(i).start()
-        load_w2(i).start()
-    load_w2j.start()
+    load_w1(0).start()
+    load_w2(0).start()
 
     barrier = pltpu.get_barrier_semaphore()
     for s in range(1, NUM_DEV):
@@ -118,19 +116,23 @@
         hrow[8 * c:8 * c + TASKS, :] = head_ref[c].astype(F32)
     head = hrow[...].astype(BF16)
 
-    pl.semaphore_wait(barrier, NUM_DEV - 1)
-    load_x.wait()
-    x_copy(0, 1).start()
-    x_copy(0, 2).start()
-    for s in range(1, NUM_DEV):
-        c_copy(s).start()
-
     block = lax.div(lax.broadcasted_iota(jnp.int32, (HEAD_ROWS, TASKS * CLASSES * 128), 1), 128)
     pick = lax.rem(block, CLASSES) * 8 + lax.div(block, CLASSES)
     ones = (lax.broadcasted_iota(jnp.int32, block.shape, 0) == pick).astype(F32).astype(BF16)
     wide = dot_nn(hrow[...].T.astype(BF16), ones)
     for k in range(TASKS * CLASSES):
         hbc[k] = wide[:, 128 * k:128 * k + 128]
+    pl.semaphore_wait(barrier, NUM_DEV - 1)
+    load_x.wait()
+    x_copy(0, 1).start()
+    x_copy(0, 2).start()
+    for s in range(1, NUM_DEV):
+        c_copy(s).start()
+    for i in range(1, NCHUNK):
+        load_w1(i).start()
+        load_w2(i).start()
+    load_w2j.start()
+
     load_w1j.wait()
     w1t[...] = w1j[...].astype(F32).T.astype(BF16)
 
@@ -197,8 +199,6 @@
         c_copy(s).wait_recv()
         total_cnt = total_cnt + cnt[s]
     inv[...] = lanes(1.0 / jnp.maximum(total_cnt, 1.0), DIM)
-    x_copy(0, 2).wait_send()
-    x_copy(0, 4).start()
 
     def tokens_ready(s):
         for k in range(1, NUM_DEV):
@@ -236,6 +236,12 @@
                 @pl.when(tp == 1)
                 def _():
                     errors_ready(s, 1 - part)
+
+                    @pl.when(s == 0)
+                    def _():
+                        x_copy(0, 2).wait_send()
+                        x_copy(0, 4).start()
+
                 run_task(s, part, 2 * tp, 0, part, 2 * tp + 1)
                 wrap = lax.div(2 * tp + 2, TASKS)
                 run_task(s, part, 2 * tp + 1, 1, part + wrap * (1 - 2 * part), 2 * tp + 2 - TASKS * wrap)
@@ -298,7 +304,7 @@
         rows = pl.ds(pl.multiple_of(dev * FEAT, FEAT), FEAT)
         return remote(gsend.at[rows, :], gx_hbm.at[me], o_send.at[s], o_recv.at[s], dev)
 
-    order = (6, 7, 4, 5, 2, 3, 1)
+    order = (2, 4, 3, 5, 6, 7, 1)
     for s in order:
         o_copy(s).start()
 

time: 127 us -> 128 us (level)
  no operation moved by 1% of the time
where the time goes in v5:
time: 128 us; the launch traced here: 127 us
  Pallas kernels  127 us (99%)
    pallas_call x1, Pallas kernels, local_step(): pl.pallas_call(kernel, out_shape=(jax.ShapeDtypeStruct((TASKS,), F32), ja...  122 us
    pallas_call x1, Pallas kernels, local_step(): pl.pallas_call(finish, out_shape=(jax.ShapeDtypeStruct((TASKS,), F32), ja...  4.24 us

profile of v5, /device:TPU:0, one launch (start us, length us, event | category | flops | bytes accessed | tf_op | source)
XLA Modules:
  0.0 127.4 jit_solution(1818779534694495179)
XLA Ops:
  0.6 122.3 %trunk.1 = (f32[4]{0:T(128)}, f32[8,96,384]{2,1,0:T(8,128)}, f32[2304,128]{1,0:T(8,128)}) custom-call(bf16[1024,768]{1,0:T(8,128)(2,1)} %x_hbm.1, bf16[768,3072]{1,0:T(8,128)(2,1)} %w_in_hbm.1, bf16[3072,768]{1,0:T(8,128)(2,1)} %w_out_hbm.1, bf16[3,4,768]{2,1,0:T(4,128)(2,1)} %bitcast.3, s32[4,1024]{1,0:T(4,128)} %lab_ref.1, s32[4,1024]{1,0:T(4,128)} %mask_ref.1), custom_call_target="tpu_custom_call" | custom-call | tf_op jit(solution)/shard_map/trunk/pallas_call | solution.py:375
  123.0 4.2 %finish.1 = (f32[4]{0:T(128)}, f32[2304,128]{1,0:T(8,128)}, f32[2304,128]{1,0:T(8,128)}) custom-call(f32[4]{0:T(128)} %get-tuple-element.9.alpha_in, f32[8,96,384]{2,1,0:T(8,128)} %get-tuple-element.10.gx_hbm, f32[2304,128]{1,0:T(8,128)} %get-tuple-element.11.g2_hbm), custom_call_target="tpu_custom_call" | custom-call | tf_op jit(solution)/shard_map/finish/pallas_call | solution.py:421

commit v6 on v5

--- a/solution.py
+++ b/solution.py
@@ -57,7 +57,7 @@
 def kernel(x_hbm, w_in_hbm, w_out_hbm, head_ref, lab_ref, mask_ref, alpha_ref, gx_hbm, out2_hbm,
            xs, w1, w2, w1j, w1t, w2j, abuf0, abuf1, zacc, hrow, hbc, ef, es, ecur, act0, act1, slope0, slope1,
            dz0, dz1, q0, q1, acc1, acc2, cnt, inv, gram, gsend, stage2,
-           x_send, x_recv, e_send, e_recv, c_send, c_recv, g_send, g_recv, o_send, o_recv, l_sem):
+           x_send, x_recv, f_send, f_recv, e_send, e_recv, c_send, c_recv, g_send, g_recv, o_send, o_recv, l_sem):
     me = lax.axis_index("data")
     core = lax.rem(me, 2)
     cx = lax.rem(lax.div(me, 2), 2)
@@ -66,26 +66,51 @@
     def flip(v, b):
         return v + b - 2 * v * b
 
-    def peer(slot):
-        hop = slot // 2
-        first, second = (1 if hop in (1, 3) else 0), (1 if hop in (2, 3) else 0)
-        bx = first * (1 - core) + second * core
-        by = first * core + second * (1 - core)
-        bc = slot % 2
-        return flip(cx, bx) * 2 + flip(cy, by) * 4 + flip(core, jnp.int32(bc))
+    def peer(s):
+        return flip(cx, s // 2 % 2) * 2 + flip(cy, s // 4) * 4 + flip(core, jnp.int32(s % 2))
 
     def remote(src, dst, send, recv, dev):
         return pltpu.make_async_remote_copy(src_ref=src, dst_ref=dst, send_sem=send, recv_sem=recv, device_id=(dev,), device_id_type=MESH)
 
-    def x_copy(src_slot, dst_slot):
-        dev = {1: 1, 2: 2, 4: 4, 3: 1, 5: 1, 6: 4, 7: 1}[dst_slot]
-        return remote(xs.at[src_slot], xs.at[dst_slot], x_send.at[dst_slot], x_recv.at[dst_slot], peer(dev))
-
-    def e_copy(slot):
-        return remote(es.at[0], es.at[slot], e_send.at[slot], e_recv.at[slot], peer(slot))
-
-    def c_copy(slot):
-        return remote(cnt.at[0], cnt.at[slot], c_send.at[slot], c_recv.at[slot], peer(slot))
+    half = pl.ds(pl.multiple_of(core * ROWS, ROWS), ROWS)
+    x_dev, y_dev = peer(2), peer(4)
+    first_dev = core * y_dev + (1 - core) * x_dev
+    second_dev = core * x_dev + (1 - core) * y_dev
+
+    def swap_copy():
+        return remote(xs.at[0], xs.at[1], x_send.at[1], x_recv.at[1], peer(1))
+
+    def hop(src, dst, i, dev):
+        return remote(xs.at[src, half, :], xs.at[dst, half, :], x_send.at[i], x_recv.at[dst], dev)
+
+    def arrived(m):
+        return hop(0, m, 2, x_dev)
+
+    hops = {
+        2: lambda: hop(0, 2 + core, 2, first_dev),
+        3: lambda: hop(1, 3 - core, 3, second_dev),
+        4: lambda: hop(1, 4 + core, 4, first_dev),
+        5: lambda: hop(0, 5 - core, 5, second_dev),
+        6: lambda: hop(2, 6, 6, y_dev),
+        7: lambda: hop(3, 7, 7, x_dev),
+    }
+
+    def hand(m):
+        return remote(xs.at[m, half, :], xs.at[m, half, :], f_send.at[m], f_recv.at[m], peer(1))
+
+    def arrival_slot(s):
+        bx, by = s // 2 % 2, s // 4
+        return 6 + core if bx and by else 2 + 2 * core if bx else 5 - 2 * core if by else 1
+
+    def e_copy(s):
+        slot = arrival_slot(s)
+        return remote(es.at[0], es.at[slot], e_send.at[s], e_recv.at[slot], peer(s))
+
+    def e_arrived(slot):
+        return remote(es.at[0], es.at[slot], e_send.at[1], e_recv.at[slot], peer(1))
+
+    def c_copy(s):
+        return remote(cnt.at[0], cnt.at[s], c_send.at[s], c_recv.at[s], peer(s))
 
     def local(src, dst, i):
         return pltpu.make_async_copy(src, dst, l_sem.at[i])
@@ -124,8 +149,8 @@
         hbc[k] = wide[:, 128 * k:128 * k + 128]
     pl.semaphore_wait(barrier, NUM_DEV - 1)
     load_x.wait()
-    x_copy(0, 1).start()
-    x_copy(0, 2).start()
+    hops[2]().start()
+    swap_copy().start()
     for s in range(1, NUM_DEV):
         c_copy(s).start()
     for i in range(1, NCHUNK):
@@ -153,6 +178,11 @@
         load_w2(h).wait()
         acc1[h] = jnp.zeros((HID, DIM), F32)
         acc2[h] = jnp.zeros((HID, DIM), F32)
+        @pl.when(h == 1)
+        def _():
+            swap_copy().wait_recv()
+            hops[3]().start()
+
         abuf0[...] = gelu_value(dot_nn(xs[0, half0, :], w1[h])).astype(BF16)
         zacc[half1, :] += dot_nn(abuf1[...], w2[jnp.maximum(h - 1, 0)])
         abuf1[...] = gelu_value(dot_nn(xs[0, half1, :], w1[h])).astype(BF16)
@@ -200,21 +230,28 @@
         total_cnt = total_cnt + cnt[s]
     inv[...] = lanes(1.0 / jnp.maximum(total_cnt, 1.0), DIM)
 
+    def tokens_pass(s):
+        for k in (0, 2, 4):
+            @pl.when(s == k)
+            def _():
+                for m in (k + 2, k + 3):
+                    arrived(m).wait_recv()
+                    hand(m).start()
+                if k < 4:
+                    for m in (k + 4, k + 5):
+                        hops[m]().start()
+
     def tokens_ready(s):
-        for k in range(1, NUM_DEV):
-            @pl.when(s == k - 1)
+        for m in range(2, NUM_DEV):
+            @pl.when(s == m - 1)
             def _():
-                x_copy(0, k).wait_recv()
-                if k == 2:
-                    x_copy(2, 6).start()
-                if k in (2, 4, 6):
-                    x_copy(k, k + 1).start()
+                hand(m).wait_recv()
 
     def errors_ready(s, part):
         for k in range(1, NUM_DEV):
             @pl.when(s == k - 1)
             def _():
-                e_copy(k).wait_recv()
+                e_arrived(k).wait_recv()
                 for t in range(TASKS):
                     ecur[part, t] = es[k, 8 * t:8 * t + 8, :].astype(F32)
 
@@ -236,11 +273,8 @@
                 @pl.when(tp == 1)
                 def _():
                     errors_ready(s, 1 - part)
-
-                    @pl.when(s == 0)
-                    def _():
-                        x_copy(0, 2).wait_send()
-                        x_copy(0, 4).start()
+                    if part == 0:
+                        tokens_pass(s)
 
                 run_task(s, part, 2 * tp, 0, part, 2 * tp + 1)
                 wrap = lax.div(2 * tp + 2, TASKS)
@@ -322,9 +356,10 @@
     for s in range(1, NUM_DEV):
         o_copy(s).wait_recv()
 
-    x_copy(0, 1).wait_send()
-    for k in (4, 3, 5, 6, 7):
-        x_copy(0, k).wait_send()
+    swap_copy().wait_send()
+    for m in range(2, NUM_DEV):
+        hops[m]().wait_send()
+        hand(m).wait_send()
     for s in range(1, NUM_DEV):
         e_copy(s).wait_send()
         c_copy(s).wait_send()
@@ -411,7 +446,7 @@
                 v((NUM_DEV, 16, 128), F32),
                 v((DIM, HID), F32),
                 v((FLAT, 128), F32),
-                sem, sem, sem, sem, sem, sem, sem, sem, sem, sem,
+                sem, sem, sem, sem, sem, sem, sem, sem, sem, sem, sem, sem,
                 pltpu.SemaphoreType.DMA((3 + 2 * NCHUNK,)),
             ],
             compiler_params=pltpu.CompilerParams(collective_id=0, has_side_effects=True, vmem_limit_bytes=66_000_000),

time: 128 us -> 125 us (0.977)
  Pallas kernels: 127 us -> 124 us
    pallas_call x1, Pallas kernels: 122 us -> 120 us  [local_step(): pl.pallas_call(kernel, out_shape=(jax.ShapeDtypeStruct((TASKS,), F32), ja...]
where the time goes in v6:
time: 125 us
  Pallas kernels  124 us (99%)
    pallas_call x1, Pallas kernels, local_step(): pl.pallas_call(kernel, out_shape=(jax.ShapeDtypeStruct((TASKS,), F32), ja...  120 us
    pallas_call x1, Pallas kernels, local_step(): pl.pallas_call(finish, out_shape=(jax.ShapeDtypeStruct((TASKS,), F32), ja...  4.24 us

profile of v6, /device:TPU:0, one launch (start us, length us, event | category | flops | bytes accessed | tf_op | source)
XLA Modules:
  0.0 124.6 jit_solution(9248109717465056087)
XLA Ops:
  0.6 119.6 %trunk.1 = (f32[4]{0:T(128)}, f32[8,96,384]{2,1,0:T(8,128)}, f32[2304,128]{1,0:T(8,128)}) custom-call(bf16[1024,768]{1,0:T(8,128)(2,1)} %x_hbm.1, bf16[768,3072]{1,0:T(8,128)(2,1)} %w_in_hbm.1, bf16[3072,768]{1,0:T(8,128)(2,1)} %w_out_hbm.1, bf16[3,4,768]{2,1,0:T(4,128)(2,1)} %bitcast.3, s32[4,1024]{1,0:T(4,128)} %lab_ref.1, s32[4,1024]{1,0:T(4,128)} %mask_ref.1), custom_call_target="tpu_custom_call" | custom-call | tf_op jit(solution)/shard_map/trunk/pallas_call | solution.py:410
  120.2 4.2 %finish.1 = (f32[4]{0:T(128)}, f32[2304,128]{1,0:T(8,128)}, f32[2304,128]{1,0:T(8,128)}) custom-call(f32[4]{0:T(128)} %get-tuple-element.9.alpha_in, f32[8,96,384]{2,1,0:T(8,128)} %get-tuple-element.10.gx_hbm, f32[2304,128]{1,0:T(8,128)} %get-tuple-element.11.g2_hbm), custom_call_target="tpu_custom_call" | custom-call | tf_op jit(solution)/shard_map/finish/pallas_call | solution.py:456

commit v7 on v6

--- a/solution.py
+++ b/solution.py
@@ -230,22 +230,24 @@
         total_cnt = total_cnt + cnt[s]
     inv[...] = lanes(1.0 / jnp.maximum(total_cnt, 1.0), DIM)
 
-    def tokens_pass(s):
-        for k in (0, 2, 4):
+    def link_half_ready(s):
+        for k in (1, 3, 5):
             @pl.when(s == k)
             def _():
-                for m in (k + 2, k + 3):
+                for m in (k + 1, k + 2):
                     arrived(m).wait_recv()
                     hand(m).start()
-                if k < 4:
-                    for m in (k + 4, k + 5):
-                        hops[m]().start()
-
-    def tokens_ready(s):
+
+    def other_half_ready(s):
         for m in range(2, NUM_DEV):
             @pl.when(s == m - 1)
             def _():
                 hand(m).wait_recv()
+        for k, after in ((0, (4, 5)), (2, (6, 7))):
+            @pl.when(s == k)
+            def _():
+                for m in after:
+                    hops[m]().start()
 
     def errors_ready(s, part):
         for k in range(1, NUM_DEV):
@@ -261,20 +263,19 @@
         qs[j][...] = (dot_nn(w2j[...], dzs[j][...]) * slopes[part][...]).astype(BF16)
         acc2[t] += (dot_nt(acts[part][...], dzs[j][...]) * scale).astype(BF16).astype(F32)
         make_dz(dzs[1 - j], next_part, next_t)
-        preact(nxt, 1 - part, t)
+        preact(nxt, 1 - part, lax.rem(t + 2 * core, TASKS))
         acc1[t] += (dot_nn(qs[j][...], xs[s]) * scale).astype(BF16).astype(F32)
 
     def shard_pair(sp, carry):
         for part in range(2):
             s = 2 * sp + part
-            tokens_ready(s)
+            link_half_ready(s)
 
             def task_pair(tp, c):
                 @pl.when(tp == 1)
                 def _():
                     errors_ready(s, 1 - part)
-                    if part == 0:
-                        tokens_pass(s)
+                    other_half_ready(s)
 
                 run_task(s, part, 2 * tp, 0, part, 2 * tp + 1)
                 wrap = lax.div(2 * tp + 2, TASKS)
@@ -375,17 +376,23 @@
 
 
 def finish(alpha_in, gx_hbm, g2_hbm, alpha_ref, out1_hbm, out2_hbm, blocks, stage1, stage2, in_sem, out_sem):
-    loads = [pltpu.make_async_copy(gx_hbm.at[d], blocks.at[d], in_sem.at[d]) for d in range(NUM_DEV)]
-    load2 = pltpu.make_async_copy(g2_hbm, stage2, in_sem.at[NUM_DEV])
-    for c in loads:
+    halves = [[pltpu.make_async_copy(gx_hbm.at[d, pl.ds(h * HALF, HALF), :], blocks.at[d, pl.ds(h * HALF, HALF), :], in_sem.at[h, d]) for d in range(NUM_DEV)] for h in range(2)]
+    load2 = pltpu.make_async_copy(g2_hbm, stage2, out_sem.at[3])
+    store2 = pltpu.make_async_copy(stage2, out2_hbm, out_sem.at[2])
+    for c in halves[0]:
         c.start()
     load2.start()
+    for c in halves[1]:
+        c.start()
     for t in range(TASKS):
         alpha_ref[t] = alpha_in[t]
-    for c in loads:
-        c.wait()
-    stores = []
+    stores = [store2]
     for h in range(2):
+        for c in halves[h]:
+            c.wait()
+        if h == 1:
+            load2.wait()
+            store2.start()
         for d in range(NUM_DEV):
             for b in range(PER):
                 first = h * HALF * (HIDDEN // 128) + d * PER + b
@@ -393,10 +400,6 @@
         rows = pl.ds(h * FLAT // 2, FLAT // 2)
         stores.append(pltpu.make_async_copy(stage1.at[rows, :], out1_hbm.at[rows, :], out_sem.at[h]))
         stores[-1].start()
-        if h == 0:
-            load2.wait()
-            stores.append(pltpu.make_async_copy(stage2, out2_hbm, out_sem.at[2]))
-            stores[-1].start()
     for c in stores:
         c.wait()
 
@@ -466,8 +469,8 @@
                 v((NUM_DEV, FEAT, HID), F32),
                 v((FLAT, 128), F32),
                 v((FLAT, 128), F32),
-                pltpu.SemaphoreType.DMA((NUM_DEV + 1,)),
-                pltpu.SemaphoreType.DMA((3,)),
+                pltpu.SemaphoreType.DMA((2, NUM_DEV)),
+                pltpu.SemaphoreType.DMA((4,)),
             ],
             name="finish",
         )(alpha, gx, g2)

time: 125 us -> 122 us (0.976)
  Pallas kernels: 124 us -> 121 us
    pallas_call x1, Pallas kernels: 120 us -> 117 us  [local_step(): pl.pallas_call(kernel, out_shape=(jax.ShapeDtypeStruct((TASKS,), F32), ja...]
where the time goes in v7:
time: 122 us
  Pallas kernels  121 us (99%)
    pallas_call x1, Pallas kernels, local_step(): pl.pallas_call(kernel, out_shape=(jax.ShapeDtypeStruct((TASKS,), F32), ja...  117 us
    pallas_call x1, Pallas kernels, local_step(): pl.pallas_call(finish, out_shape=(jax.ShapeDtypeStruct((TASKS,), F32), ja...  4.29 us

profile of v7, /device:TPU:0, one launch (start us, length us, event | category | flops | bytes accessed | tf_op | source)
XLA Modules:
  0.0 122.0 jit_solution(11112218479368127354)
XLA Ops:
  0.6 116.9 %trunk.1 = (f32[4]{0:T(128)}, f32[8,96,384]{2,1,0:T(8,128)}, f32[2304,128]{1,0:T(8,128)}) custom-call(bf16[1024,768]{1,0:T(8,128)(2,1)} %x_hbm.1, bf16[768,3072]{1,0:T(8,128)(2,1)} %w_in_hbm.1, bf16[3072,768]{1,0:T(8,128)(2,1)} %w_out_hbm.1, bf16[3,4,768]{2,1,0:T(4,128)(2,1)} %bitcast.3, s32[4,1024]{1,0:T(4,128)} %lab_ref.1, s32[4,1024]{1,0:T(4,128)} %mask_ref.1), custom_call_target="tpu_custom_call" | custom-call | tf_op jit(solution)/shard_map/trunk/pallas_call | solution.py:413
  117.5 4.3 %finish.1 = (f32[4]{0:T(128)}, f32[2304,128]{1,0:T(8,128)}, f32[2304,128]{1,0:T(8,128)}) custom-call(f32[4]{0:T(128)} %get-tuple-element.9.alpha_in, f32[8,96,384]{2,1,0:T(8,128)} %get-tuple-element.10.gx_hbm, f32[2304,128]{1,0:T(8,128)} %get-tuple-element.11.g2_hbm), custom_call_target="tpu_custom_call" | custom-call | tf_op jit(solution)/shard_map/finish/pallas_call | solution.py:459

commit v8 on v7

--- a/solution.py
+++ b/solution.py
@@ -54,9 +54,9 @@
     return p * cdf, slope
 
 
-def kernel(x_hbm, w_in_hbm, w_out_hbm, head_ref, lab_ref, mask_ref, alpha_ref, gx_hbm, out2_hbm,
+def kernel(x_hbm, w_in_hbm, w_out_hbm, head_ref, lab_ref, mask_ref, alpha_ref, gx, stage2,
            xs, w1, w2, w1j, w1t, w2j, abuf0, abuf1, zacc, hrow, hbc, ef, es, ecur, act0, act1, slope0, slope1,
-           dz0, dz1, q0, q1, acc1, acc2, cnt, inv, gram, gsend, stage2,
+           dz0, dz1, q0, q1, acc1, acc2, cnt, inv, gram, gsend,
            x_send, x_recv, f_send, f_recv, e_send, e_recv, c_send, c_recv, g_send, g_recv, o_send, o_recv, l_sem):
     me = lax.axis_index("data")
     core = lax.rem(me, 2)
@@ -325,7 +325,7 @@
         norm = (raised[0] + raised[1]) + (raised[2] + raised[3])
         al = [r / norm for r in raised]
     for t in range(TASKS):
-        alpha_ref[t] = jnp.max(al[t])
+        alpha_ref[t:t + 1, :] = al[t]
 
     for c in range(DIM // 128):
         cols = slice(128 * c, 128 * c + 128)
@@ -337,7 +337,7 @@
     def o_copy(s):
         dev = peer(s)
         rows = pl.ds(pl.multiple_of(dev * FEAT, FEAT), FEAT)
-        return remote(gsend.at[rows, :], gx_hbm.at[me], o_send.at[s], o_recv.at[s], dev)
+        return remote(gsend.at[rows, :], gx.at[me], o_send.at[s], o_recv.at[s], dev)
 
     order = (2, 4, 3, 5, 6, 7, 1)
     for s in order:
@@ -349,11 +349,8 @@
         for t in range(1, TASKS):
             comb = comb + al[t] * acc2[t, :, cols]
         stage2[pl.ds(c, HID, stride=DIM // 128), :] = comb
-    store2 = local(stage2, out2_hbm, 0)
-    store2.start()
-
-    keep = local(gsend.at[pl.ds(pl.multiple_of(me * FEAT, FEAT), FEAT), :], gx_hbm.at[me], 1)
-    keep.start()
+
+    gx[me] = gsend[pl.ds(pl.multiple_of(me * FEAT, FEAT), FEAT), :]
     for s in range(1, NUM_DEV):
         o_copy(s).wait_recv()
 
@@ -366,8 +363,6 @@
         c_copy(s).wait_send()
         gram_copy(s, me).wait_send()
         o_copy(s).wait_send()
-    store2.wait()
-    keep.wait()
 
 
 PER = HID // 128
@@ -375,24 +370,12 @@
 HALF = FEAT // 2
 
 
-def finish(alpha_in, gx_hbm, g2_hbm, alpha_ref, out1_hbm, out2_hbm, blocks, stage1, stage2, in_sem, out_sem):
-    halves = [[pltpu.make_async_copy(gx_hbm.at[d, pl.ds(h * HALF, HALF), :], blocks.at[d, pl.ds(h * HALF, HALF), :], in_sem.at[h, d]) for d in range(NUM_DEV)] for h in range(2)]
-    load2 = pltpu.make_async_copy(g2_hbm, stage2, out_sem.at[3])
-    store2 = pltpu.make_async_copy(stage2, out2_hbm, out_sem.at[2])
-    for c in halves[0]:
-        c.start()
-    load2.start()
-    for c in halves[1]:
-        c.start()
+def finish(alpha_in, blocks, stage2, alpha_ref, out1_hbm, out2_hbm, stage1, out_sem):
+    stores = [pltpu.make_async_copy(stage2, out2_hbm, out_sem.at[2])]
+    stores[0].start()
     for t in range(TASKS):
-        alpha_ref[t] = alpha_in[t]
-    stores = [store2]
+        alpha_ref[t] = jnp.max(alpha_in[t:t + 1, :])
     for h in range(2):
-        for c in halves[h]:
-            c.wait()
-        if h == 1:
-            load2.wait()
-            store2.start()
         for d in range(NUM_DEV):
             for b in range(PER):
                 first = h * HALF * (HIDDEN // 128) + d * PER + b
@@ -413,12 +396,12 @@
         alpha, gx, g2 = pl.pallas_call(
             kernel,
             out_shape=(
-                jax.ShapeDtypeStruct((TASKS,), F32),
-                jax.ShapeDtypeStruct((NUM_DEV, FEAT, HID), F32),
-                jax.ShapeDtypeStruct((FLAT, 128), F32),
+                v((TASKS, 128), F32),
+                v((NUM_DEV, FEAT, HID), F32),
+                v((FLAT, 128), F32),
             ),
             in_specs=[hbm, hbm, hbm, vmem, vmem, vmem],
-            out_specs=(pl.BlockSpec(memory_space=pltpu.SMEM), hbm, hbm),
+            out_specs=(vmem, vmem, vmem),
             scratch_shapes=[
                 v((NUM_DEV, TOK, DIM), BF16),
                 v((NCHUNK, DIM, CHUNK), BF16),
@@ -448,11 +431,10 @@
                 v((8, DIM), F32),
                 v((NUM_DEV, 16, 128), F32),
                 v((DIM, HID), F32),
-                v((FLAT, 128), F32),
                 sem, sem, sem, sem, sem, sem, sem, sem, sem, sem, sem, sem,
                 pltpu.SemaphoreType.DMA((3 + 2 * NCHUNK,)),
             ],
-            compiler_params=pltpu.CompilerParams(collective_id=0, has_side_effects=True, vmem_limit_bytes=66_000_000),
+            compiler_params=pltpu.CompilerParams(collective_id=0, has_side_effects=True, vmem_limit_bytes=62_000_000),
             name="trunk",
         )(x_loc, w_in, w_out, heads.transpose(2, 0, 1), lab_loc, mask_loc)
         smem = pl.BlockSpec(memory_space=pltpu.SMEM)
@@ -463,15 +445,13 @@
                 jax.ShapeDtypeStruct((FLAT, 128), F32),
                 jax.ShapeDtypeStruct((FLAT, 128), F32),
             ),
-            in_specs=[smem, hbm, hbm],
+            in_specs=[vmem, vmem, vmem],
             out_specs=(smem, hbm, hbm),
             scratch_shapes=[
-                v((NUM_DEV, FEAT, HID), F32),
                 v((FLAT, 128), F32),
-                v((FLAT, 128), F32),
-                pltpu.SemaphoreType.DMA((2, NUM_DEV)),
-                pltpu.SemaphoreType.DMA((4,)),
+                pltpu.SemaphoreType.DMA((3,)),
             ],
+            compiler_params=pltpu.CompilerParams(vmem_limit_bytes=8_000_000),
             name="finish",
         )(alpha, gx, g2)
         return alpha, out1.reshape(-1), out2.reshape(-1)

time: 122 us -> 119 us (0.975)
  Pallas kernels: 121 us -> 118 us
    pallas_call x1, Pallas kernels: 4.29 us -> 1.94 us  [local_step(): pl.pallas_call(finish, out_shape=(jax.ShapeDtypeStruct((TASKS,), F32), ja...]
where the time goes in v8:
time: 119 us
  Pallas kernels  118 us (99%)
    pallas_call x1, Pallas kernels, local_step(): pl.pallas_call(kernel, out_shape=(v((TASKS, 128), F32), v((NUM_DEV, FEAT,...  116 us

profile of v8, /device:TPU:0, one launch (start us, length us, event | category | flops | bytes accessed | tf_op | source)
XLA Modules:
  0.0 119.1 jit_solution(14614340844354346165)
XLA Ops:
  0.6 116.4 %trunk.1 = (f32[4,128]{1,0:T(4,128)S(1)}, f32[8,96,384]{2,1,0:T(8,128)S(1)}, f32[2304,128]{1,0:T(8,128)S(1)}) custom-call(bf16[1024,768]{1,0:T(8,128)(2,1)} %x_hbm.1, bf16[768,3072]{1,0:T(8,128)(2,1)} %w_in_hbm.1, bf16[3072,768]{1,0:T(8,128)(2,1)} %w_out_hbm.1, bf16[3,4,768]{2,1,0:T(4,128)(2,1)} %bitcast.3, s32[4,1024]{1,0:T(4,128)} %lab_ref.1, ...), custom_call_target="tpu_custom_call" | custom-call | tf_op jit(solution)/shard_map/trunk/pallas_call | solution.py:396
  117.0 1.9 %finish.1 = (f32[4]{0:T(128)}, f32[2304,128]{1,0:T(8,128)}, f32[2304,128]{1,0:T(8,128)}) custom-call(f32[4,128]{1,0:T(4,128)S(1)} %get-tuple-element.9.alpha_in, f32[8,96,384]{2,1,0:T(8,128)S(1)} %get-tuple-element.10.blocks, f32[2304,128]{1,0:T(8,128)S(1)} %get-tuple-element.11.stage2), custom_call_target="tpu_custom_call" | custom-call | tf_op jit(solution)/shard_map/finish/pallas_call | solution.py:441

commit v9 on v8

--- a/solution.py
+++ b/solution.py
@@ -91,8 +91,8 @@
         3: lambda: hop(1, 3 - core, 3, second_dev),
         4: lambda: hop(1, 4 + core, 4, first_dev),
         5: lambda: hop(0, 5 - core, 5, second_dev),
-        6: lambda: hop(2, 6, 6, y_dev),
-        7: lambda: hop(3, 7, 7, x_dev),
+        6: lambda: hop(2 + 3 * core, 6, 6, second_dev),
+        7: lambda: hop(4 - core, 7, 7, second_dev),
     }
 
     def hand(m):
@@ -231,23 +231,26 @@
     inv[...] = lanes(1.0 / jnp.maximum(total_cnt, 1.0), DIM)
 
     def link_half_ready(s):
-        for k in (1, 3, 5):
+        for k, slots in ((1, (2, 3)), (3, (4, 5)), (5, (6,)), (6, (7,))):
             @pl.when(s == k)
             def _():
-                for m in (k + 1, k + 2):
+                for m in slots:
                     arrived(m).wait_recv()
                     hand(m).start()
+                if k == 3:
+                    hops[6]().start()
+                    hops[7]().start()
 
     def other_half_ready(s):
         for m in range(2, NUM_DEV):
             @pl.when(s == m - 1)
             def _():
                 hand(m).wait_recv()
-        for k, after in ((0, (4, 5)), (2, (6, 7))):
-            @pl.when(s == k)
-            def _():
-                for m in after:
-                    hops[m]().start()
+
+        @pl.when(s == 0)
+        def _():
+            hops[4]().start()
+            hops[5]().start()
 
     def errors_ready(s, part):
         for k in range(1, NUM_DEV):

time: 119 us -> 119 us (level)
  no operation moved by 1% of the time
where the time goes in v9:
time: 119 us
  Pallas kernels  118 us (99%)
    pallas_call x1, Pallas kernels, local_step(): pl.pallas_call(kernel, out_shape=(v((TASKS, 128), F32), v((NUM_DEV, FEAT,...  116 us

profile of v9, /device:TPU:0, one launch (start us, length us, event | category | flops | bytes accessed | tf_op | source)
XLA Modules:
  0.0 119.1 jit_solution(17884820466468392385)
XLA Ops:
  0.6 116.3 %trunk.1 = (f32[4,128]{1,0:T(4,128)S(1)}, f32[8,96,384]{2,1,0:T(8,128)S(1)}, f32[2304,128]{1,0:T(8,128)S(1)}) custom-call(bf16[1024,768]{1,0:T(8,128)(2,1)} %x_hbm.1, bf16[768,3072]{1,0:T(8,128)(2,1)} %w_in_hbm.1, bf16[3072,768]{1,0:T(8,128)(2,1)} %w_out_hbm.1, bf16[3,4,768]{2,1,0:T(4,128)(2,1)} %bitcast.3, s32[4,1024]{1,0:T(4,128)} %lab_ref.1, ...), custom_call_target="tpu_custom_call" | custom-call | tf_op jit(solution)/shard_map/trunk/pallas_call | solution.py:399
  117.0 1.9 %finish.1 = (f32[4]{0:T(128)}, f32[2304,128]{1,0:T(8,128)}, f32[2304,128]{1,0:T(8,128)}) custom-call(f32[4,128]{1,0:T(4,128)S(1)} %get-tuple-element.9.alpha_in, f32[8,96,384]{2,1,0:T(8,128)S(1)} %get-tuple-element.10.blocks, f32[2304,128]{1,0:T(8,128)S(1)} %get-tuple-element.11.stage2), custom_call_target="tpu_custom_call" | custom-call | tf_op jit(solution)/shard_map/finish/pallas_call | solution.py:444

commit v10 on v9

--- a/solution.py
+++ b/solution.py
@@ -17,6 +17,7 @@
 HID = HIDDEN // NUM_DEV
 FEAT = DIM // NUM_DEV
 HEAD_ROWS = 32
+PITCH = TOK + 128
 CHUNK = 768
 ROWS = 512
 NCHUNK = HIDDEN // CHUNK
@@ -218,7 +219,7 @@
         for k in range(DIM // 8):
             f = slice(8 * k, 8 * k + 8)
             h = [lanes(hbc[CLASSES * t + c, f, :], TOK) for c in range(CLASSES)]
-            dst[f, :] = (h[0] * rows[0] + h[1] * rows[1] + h[2] * rows[2]).astype(BF16)
+            dst[f, 0:TOK] = (h[0] * rows[0] + h[1] * rows[1] + h[2] * rows[2]).astype(BF16)
 
     for s in range(1, NUM_DEV):
         e_copy(s).start()
@@ -263,11 +264,11 @@
     def run_task(s, part, t, j, next_part, next_t):
         nxt = jnp.minimum(s + 1, NUM_DEV - 1)
         scale = inv[pl.ds(t, 1), :]
-        qs[j][...] = (dot_nn(w2j[...], dzs[j][...]) * slopes[part][...]).astype(BF16)
-        acc2[t] += (dot_nt(acts[part][...], dzs[j][...]) * scale).astype(BF16).astype(F32)
+        qs[j][:, 0:TOK] = (dot_nn(w2j[...], dzs[j][:, 0:TOK]) * slopes[part][...]).astype(BF16)
+        acc2[t] += (dot_nt(acts[part][:, 0:TOK], dzs[j][:, 0:TOK]) * scale).astype(BF16).astype(F32)
         make_dz(dzs[1 - j], next_part, next_t)
         preact(nxt, 1 - part, lax.rem(t + 2 * core, TASKS))
-        acc1[t] += (dot_nn(qs[j][...], xs[s]) * scale).astype(BF16).astype(F32)
+        acc1[t] += (dot_nn(qs[j][:, 0:TOK], xs[s]) * scale).astype(BF16).astype(F32)
 
     def shard_pair(sp, carry):
         for part in range(2):
@@ -420,14 +421,14 @@
                 v((HEAD_ROWS, TOK), F32),
                 v((NUM_DEV, HEAD_ROWS, TOK), BF16),
                 v((2, TASKS, 8, TOK), F32),
-                v((HID, TOK), BF16),
-                v((HID, TOK), BF16),
+                v((HID, PITCH), BF16),
+                v((HID, PITCH), BF16),
                 v((HID, TOK), F32),
                 v((HID, TOK), F32),
-                v((DIM, TOK), BF16),
-                v((DIM, TOK), BF16),
-                v((HID, TOK), BF16),
-                v((HID, TOK), BF16),
+                v((DIM, PITCH), BF16),
+                v((DIM, PITCH), BF16),
+                v((HID, PITCH), BF16),
+                v((HID, PITCH), BF16),
                 v((TASKS, HID, DIM), F32),
                 v((TASKS, HID, DIM), F32),
                 v((NUM_DEV, 8, 128), F32),

time: 119 us -> 119 us (level)
  no operation moved by 1% of the time
where the time goes in v10:
time: 119 us
  Pallas kernels  118 us (99%)
    pallas_call x1, Pallas kernels, local_step(): pl.pallas_call(kernel, out_shape=(v((TASKS, 128), F32), v((NUM_DEV, FEAT,...  116 us

profile of v10, /device:TPU:0, one launch (start us, length us, event | category | flops | bytes accessed | tf_op | source)
XLA Modules:
  0.0 118.9 jit_solution(4385525441892733069)
XLA Ops:
  0.6 116.1 %trunk.1 = (f32[4,128]{1,0:T(4,128)S(1)}, f32[8,96,384]{2,1,0:T(8,128)S(1)}, f32[2304,128]{1,0:T(8,128)S(1)}) custom-call(bf16[1024,768]{1,0:T(8,128)(2,1)} %x_hbm.1, bf16[768,3072]{1,0:T(8,128)(2,1)} %w_in_hbm.1, bf16[3072,768]{1,0:T(8,128)(2,1)} %w_out_hbm.1, bf16[3,4,768]{2,1,0:T(4,128)(2,1)} %bitcast.3, s32[4,1024]{1,0:T(4,128)} %lab_ref.1, ...), custom_call_target="tpu_custom_call" | custom-call | tf_op jit(solution)/shard_map/trunk/pallas_call | solution.py:400
  116.7 1.9 %finish.1 = (f32[4]{0:T(128)}, f32[2304,128]{1,0:T(8,128)}, f32[2304,128]{1,0:T(8,128)}) custom-call(f32[4,128]{1,0:T(4,128)S(1)} %get-tuple-element.9.alpha_in, f32[8,96,384]{2,1,0:T(8,128)S(1)} %get-tuple-element.10.blocks, f32[2304,128]{1,0:T(8,128)S(1)} %get-tuple-element.11.stage2), custom_call_target="tpu_custom_call" | custom-call | tf_op jit(solution)/shard_map/finish/pallas_call | solution.py:445

commit v11 on v10

--- a/solution.py
+++ b/solution.py
@@ -248,11 +248,6 @@
             def _():
                 hand(m).wait_recv()
 
-        @pl.when(s == 0)
-        def _():
-            hops[4]().start()
-            hops[5]().start()
-
     def errors_ready(s, part):
         for k in range(1, NUM_DEV):
             @pl.when(s == k - 1)
@@ -289,6 +284,8 @@
             lax.fori_loop(0, TASKS // 2, task_pair, 0)
         return carry
 
+    hops[4]().start()
+    hops[5]().start()
     lax.fori_loop(0, NUM_DEV // 2, shard_pair, 0)
 
     def gram_rows(i, sums):

time: 119 us -> 119 us (level)
  no operation moved by 1% of the time
where the time goes in v11:
time: 119 us
  Pallas kernels  118 us (99%)
    pallas_call x1, Pallas kernels, local_step(): pl.pallas_call(kernel, out_shape=(v((TASKS, 128), F32), v((NUM_DEV, FEAT,...  116 us

profile of v11, /device:TPU:0, one launch (start us, length us, event | category | flops | bytes accessed | tf_op | source)
XLA Modules:
  0.0 118.8 jit_solution(9009545148271001211)
XLA Ops:
  0.6 116.0 %trunk.1 = (f32[4,128]{1,0:T(4,128)S(1)}, f32[8,96,384]{2,1,0:T(8,128)S(1)}, f32[2304,128]{1,0:T(8,128)S(1)}) custom-call(bf16[1024,768]{1,0:T(8,128)(2,1)} %x_hbm.1, bf16[768,3072]{1,0:T(8,128)(2,1)} %w_in_hbm.1, bf16[3072,768]{1,0:T(8,128)(2,1)} %w_out_hbm.1, bf16[3,4,768]{2,1,0:T(4,128)(2,1)} %bitcast.3, s32[4,1024]{1,0:T(4,128)} %lab_ref.1, ...), custom_call_target="tpu_custom_call" | custom-call | tf_op jit(solution)/shard_map/trunk/pallas_call | solution.py:397
  116.7 1.9 %finish.1 = (f32[4]{0:T(128)}, f32[2304,128]{1,0:T(8,128)}, f32[2304,128]{1,0:T(8,128)}) custom-call(f32[4,128]{1,0:T(4,128)S(1)} %get-tuple-element.9.alpha_in, f32[8,96,384]{2,1,0:T(8,128)S(1)} %get-tuple-element.10.blocks, f32[2304,128]{1,0:T(8,128)S(1)} %get-tuple-element.11.stage2), custom_call_target="tpu_custom_call" | custom-call | tf_op jit(solution)/shard_map/finish/pallas_call | solution.py:442

commit v12 on v11

--- a/solution.py
+++ b/solution.py
@@ -55,8 +55,8 @@
     return p * cdf, slope
 
 
-def kernel(x_hbm, w_in_hbm, w_out_hbm, head_ref, lab_ref, mask_ref, alpha_ref, gx, stage2,
-           xs, w1, w2, w1j, w1t, w2j, abuf0, abuf1, zacc, hrow, hbc, ef, es, ecur, act0, act1, slope0, slope1,
+def kernel(x_hbm, w_in_hbm, w_out_hbm, head_hbm, lab_hbm, mask_hbm, alpha_ref, gx, stage2,
+           head_ref, lab_ref, mask_ref, xs, w1, w2, w1j, w1t, w2j, abuf0, abuf1, zacc, hrow, hbc, ef, es, ecur, act0, act1, slope0, slope1,
            dz0, dz1, q0, q1, acc1, acc2, cnt, inv, gram, gsend,
            x_send, x_recv, f_send, f_recv, e_send, e_recv, c_send, c_recv, g_send, g_recv, o_send, o_recv, l_sem):
     me = lax.axis_index("data")
@@ -125,7 +125,13 @@
     load_x = local(x_hbm, xs.at[0], 0)
     load_w1j = local(w_in_hbm.at[:, pl.ds(pl.multiple_of(me * HID, HID), HID)], w1j, 1)
     load_w2j = local(w_out_hbm.at[pl.ds(pl.multiple_of(me * HID, HID), HID), :], w2j, 2)
+    load_head = local(head_hbm, head_ref, 3 + 2 * NCHUNK)
+    load_lab = local(lab_hbm, lab_ref, 4 + 2 * NCHUNK)
+    load_mask = local(mask_hbm, mask_ref, 5 + 2 * NCHUNK)
     load_x.start()
+    load_head.start()
+    load_mask.start()
+    load_lab.start()
     load_w1j.start()
     load_w1(0).start()
     load_w2(0).start()
@@ -134,9 +140,7 @@
     for s in range(1, NUM_DEV):
         pl.semaphore_signal(barrier, inc=1, device_id=(peer(s),), device_id_type=MESH)
 
-    counts = jnp.sum(mask_ref[...].astype(F32), axis=1, keepdims=True)
-    cnt[0, 0:TASKS, :] = jnp.broadcast_to(counts, (TASKS, 128))
-    cnt[0, TASKS:8, :] = jnp.zeros((8 - TASKS, 128), F32)
+    load_head.wait()
     hrow[...] = jnp.zeros_like(hrow)
     for c in range(CLASSES):
         hrow[8 * c:8 * c + TASKS, :] = head_ref[c].astype(F32)
@@ -148,19 +152,24 @@
     wide = dot_nn(hrow[...].T.astype(BF16), ones)
     for k in range(TASKS * CLASSES):
         hbc[k] = wide[:, 128 * k:128 * k + 128]
-    pl.semaphore_wait(barrier, NUM_DEV - 1)
     load_x.wait()
-    hops[2]().start()
-    swap_copy().start()
-    for s in range(1, NUM_DEV):
-        c_copy(s).start()
     for i in range(1, NCHUNK):
         load_w1(i).start()
         load_w2(i).start()
     load_w2j.start()
-
+    load_mask.wait()
+    load_lab.wait()
+    counts = jnp.sum(mask_ref[...].astype(F32), axis=1, keepdims=True)
+    cnt[0, 0:TASKS, :] = jnp.broadcast_to(counts, (TASKS, 128))
+    cnt[0, TASKS:8, :] = jnp.zeros((8 - TASKS, 128), F32)
     load_w1j.wait()
     w1t[...] = w1j[...].astype(F32).T.astype(BF16)
+
+    pl.semaphore_wait(barrier, NUM_DEV - 1)
+    hops[2]().start()
+    swap_copy().start()
+    for s in range(1, NUM_DEV):
+        c_copy(s).start()
 
     abuf1[...] = jnp.zeros_like(abuf1)
     zacc[...] = xs[0].astype(F32)
@@ -401,9 +410,12 @@
                 v((NUM_DEV, FEAT, HID), F32),
                 v((FLAT, 128), F32),
             ),
-            in_specs=[hbm, hbm, hbm, vmem, vmem, vmem],
+            in_specs=[hbm, hbm, hbm, hbm, hbm, hbm],
             out_specs=(vmem, vmem, vmem),
             scratch_shapes=[
+                v((CLASSES, TASKS, DIM), BF16),
+                v((TASKS, TOK), jnp.int32),
+                v((TASKS, TOK), jnp.int32),
                 v((NUM_DEV, TOK, DIM), BF16),
                 v((NCHUNK, DIM, CHUNK), BF16),
                 v((NCHUNK, CHUNK, DIM), BF16),
@@ -433,7 +445,7 @@
                 v((NUM_DEV, 16, 128), F32),
                 v((DIM, HID), F32),
                 sem, sem, sem, sem, sem, sem, sem, sem, sem, sem, sem, sem,
-                pltpu.SemaphoreType.DMA((3 + 2 * NCHUNK,)),
+                pltpu.SemaphoreType.DMA((6 + 2 * NCHUNK,)),
             ],
             compiler_params=pltpu.CompilerParams(collective_id=0, has_side_effects=True, vmem_limit_bytes=62_000_000),
             name="trunk",

time: 119 us -> 123 us (1.034)
  Pallas kernels: 118 us -> 122 us
    pallas_call x1, Pallas kernels: 116 us -> 120 us  [local_step(): pl.pallas_call(kernel, out_shape=(v((TASKS, 128), F32), v((NUM_DEV, FEAT,...]
where the time goes in v12:
time: 123 us
  Pallas kernels  122 us (99%)
    pallas_call x1, Pallas kernels, local_step(): pl.pallas_call(kernel, out_shape=(v((TASKS, 128), F32), v((NUM_DEV, FEAT,...  120 us

profile of v12, /device:TPU:0, one launch (start us, length us, event | category | flops | bytes accessed | tf_op | source)
XLA Modules:
  0.0 122.6 jit_solution(11443153779986027527)
XLA Ops:
  0.6 119.8 %trunk.1 = (f32[4,128]{1,0:T(4,128)S(1)}, f32[8,96,384]{2,1,0:T(8,128)S(1)}, f32[2304,128]{1,0:T(8,128)S(1)}) custom-call(bf16[1024,768]{1,0:T(8,128)(2,1)} %x_hbm.1, bf16[768,3072]{1,0:T(8,128)(2,1)} %w_in_hbm.1, bf16[3072,768]{1,0:T(8,128)(2,1)} %w_out_hbm.1, bf16[3,4,768]{2,1,0:T(4,128)(2,1)} %bitcast.3, s32[4,1024]{1,0:T(4,128)} %lab_hbm.1, ...), custom_call_target="tpu_custom_call" | custom-call | tf_op jit(solution)/shard_map/trunk/pallas_call | solution.py:406
  120.5 1.9 %finish.1 = (f32[4]{0:T(128)}, f32[2304,128]{1,0:T(8,128)}, f32[2304,128]{1,0:T(8,128)}) custom-call(f32[4,128]{1,0:T(4,128)S(1)} %get-tuple-element.9.alpha_in, f32[8,96,384]{2,1,0:T(8,128)S(1)} %get-tuple-element.10.blocks, f32[2304,128]{1,0:T(8,128)S(1)} %get-tuple-element.11.stage2), custom_call_target="tpu_custom_call" | custom-call | tf_op jit(solution)/shard_map/finish/pallas_call | solution.py:454

commit v13 on v11

--- a/solution.py
+++ b/solution.py
@@ -79,7 +79,7 @@
     second_dev = core * x_dev + (1 - core) * y_dev
 
     def swap_copy():
-        return remote(xs.at[0], xs.at[1], x_send.at[1], x_recv.at[1], peer(1))
+        return remote(x_hbm, xs.at[1], x_send.at[1], x_recv.at[1], peer(1))
 
     def hop(src, dst, i, dev):
         return remote(xs.at[src, half, :], xs.at[dst, half, :], x_send.at[i], x_recv.at[dst], dev)
@@ -88,7 +88,7 @@
         return hop(0, m, 2, x_dev)
 
     hops = {
-        2: lambda: hop(0, 2 + core, 2, first_dev),
+        2: lambda: remote(x_hbm.at[half, :], xs.at[2 + core, half, :], x_send.at[2], x_recv.at[2 + core], first_dev),
         3: lambda: hop(1, 3 - core, 3, second_dev),
         4: lambda: hop(1, 4 + core, 4, first_dev),
         5: lambda: hop(0, 5 - core, 5, second_dev),
@@ -142,18 +142,19 @@
         hrow[8 * c:8 * c + TASKS, :] = head_ref[c].astype(F32)
     head = hrow[...].astype(BF16)
 
+    pl.semaphore_wait(barrier, NUM_DEV - 1)
+    hops[2]().start()
+    swap_copy().start()
+    for s in range(1, NUM_DEV):
+        c_copy(s).start()
+
     block = lax.div(lax.broadcasted_iota(jnp.int32, (HEAD_ROWS, TASKS * CLASSES * 128), 1), 128)
     pick = lax.rem(block, CLASSES) * 8 + lax.div(block, CLASSES)
     ones = (lax.broadcasted_iota(jnp.int32, block.shape, 0) == pick).astype(F32).astype(BF16)
     wide = dot_nn(hrow[...].T.astype(BF16), ones)
     for k in range(TASKS * CLASSES):
         hbc[k] = wide[:, 128 * k:128 * k + 128]
-    pl.semaphore_wait(barrier, NUM_DEV - 1)
     load_x.wait()
-    hops[2]().start()
-    swap_copy().start()
-    for s in range(1, NUM_DEV):
-        c_copy(s).start()
     for i in range(1, NCHUNK):
         load_w1(i).start()
         load_w2(i).start()

time: 119 us -> 118 us (level)
    pallas_call x1, Pallas kernels: 116 us -> 115 us  [local_step(): pl.pallas_call(kernel, out_shape=(v((TASKS, 128), F32), v((NUM_DEV, FEAT,...]
where the time goes in v13:
time: 118 us
  Pallas kernels  117 us (99%)
    pallas_call x1, Pallas kernels, local_step(): pl.pallas_call(kernel, out_shape=(v((TASKS, 128), F32), v((NUM_DEV, FEAT,...  115 us

profile of v13, /device:TPU:0, one launch (start us, length us, event | category | flops | bytes accessed | tf_op | source)
XLA Modules:
  0.0 117.6 jit_solution(3668158186298525441)
XLA Ops:
  0.6 114.8 %trunk.1 = (f32[4,128]{1,0:T(4,128)S(1)}, f32[8,96,384]{2,1,0:T(8,128)S(1)}, f32[2304,128]{1,0:T(8,128)S(1)}) custom-call(bf16[1024,768]{1,0:T(8,128)(2,1)} %x_hbm.1, bf16[768,3072]{1,0:T(8,128)(2,1)} %w_in_hbm.1, bf16[3072,768]{1,0:T(8,128)(2,1)} %w_out_hbm.1, bf16[3,4,768]{2,1,0:T(4,128)(2,1)} %bitcast.3, s32[4,1024]{1,0:T(4,128)} %lab_ref.1, ...), custom_call_target="tpu_custom_call" | custom-call | tf_op jit(solution)/shard_map/trunk/pallas_call | solution.py:398
  115.5 1.9 %finish.1 = (f32[4]{0:T(128)}, f32[2304,128]{1,0:T(8,128)}, f32[2304,128]{1,0:T(8,128)}) custom-call(f32[4,128]{1,0:T(4,128)S(1)} %get-tuple-element.9.alpha_in, f32[8,96,384]{2,1,0:T(8,128)S(1)} %get-tuple-element.10.blocks, f32[2304,128]{1,0:T(8,128)S(1)} %get-tuple-element.11.stage2), custom_call_target="tpu_custom_call" | custom-call | tf_op jit(solution)/shard_map/finish/pallas_call | solution.py:443
